TPU v7x, 32 devices: a whole 2x2x4 slice. The times are simulated.
32 devices in a mesh: grp: 2 (over x), row: 16 (over z, y, core).
Axes of the slice: x: 2, y: 2, z: 4, core: 2. Of those that a mesh axis runs over, the one named last changes fastest.
Arguments:
- slc: bfloat16 [2, 300, 64, 256], P(None, None, ('grp', 'row')), parts along dimension 2, may hold values from -8 to 8
- mask: int32 [25, 64, 256], P(None, ('grp', 'row')), parts along dimension 1, may hold values 0 or 1
- ref_index: int32 [2], P('grp'), parts along dimension 0, may hold values from 0 to 8191
Outputs:
- linked: float32 [2, 300, 64, 256], P(None, None, ('grp', 'row')), parts along dimension 2
There are 2 independent parts, one for each index of `grp`. A program takes and returns all parts, laid end to end along the dimension named above; each array names one. Nothing has to cross between parts.
All inputs are finite; a program needn't handle non-finite values. No bound on the sum of `mask` on one device may be relied on, other than what follows from the above.
Results may differ from a plain program's by a relative error of at most 0.0046.
Values may be sent and summed in bfloat16 or wider, within the bound.
A program may use at most 64 MiB of HBM per device.

v0:
```python
import jax
import jax.numpy as jnp
from jax import lax
from jax.experimental import pallas as pl
from jax.experimental.pallas import tpu as pltpu
from jax.sharding import PartitionSpec as P

HALF = 2
ITERS = 2
WIDTH = 2 * HALF + 1
LANE = 128
SUB = 16
MESH = pl.DeviceIdType.MESH


def round_up(value, unit):
    return (value + unit - 1) // unit * unit


def row_of(column_sums):
    return jnp.sum(column_sums.T, axis=0, keepdims=True)


def kernel(
    n, ndate, total_rows, x_ref, mask_ref, index_ref, out_ref,
    low, high, flat, turned, weight, coef, total, column, powers, refs,
    low_sem, high_sem, power_sem, ref_sem,
):
    rows, depth, cols = x_ref.shape
    half_depth = depth // 2
    blocks = cols // LANE
    long_dates = powers.shape[2]
    long_depth = refs.shape[2]
    me = lax.axis_index("row")
    first_row = me * rows

    def peer(k):
        return lax.rem(me + k, n)

    barrier = pltpu.get_barrier_semaphore()

    @pl.loop(1, n)
    def _(k):
        pl.semaphore_signal(barrier, inc=1, device_id={"row": peer(k)}, device_id_type=MESH)

    column[...] = jnp.zeros_like(column)
    sums = jnp.zeros((half_depth, LANE), jnp.float32)
    for r in range(rows):
        for part in range(2):
            for block in range(blocks):
                piece = x_ref[r, part * half_depth:(part + 1) * half_depth, block * LANE:(block + 1) * LANE]
                piece = piece.astype(jnp.float32)
                sums = sums + piece * piece
    column[0:half_depth, :] = sums
    powers[me] = row_of(column[0:long_dates, :])

    pl.semaphore_wait(barrier, n - 1)

    def exchange(buffer, sems):
        def copy(k, slot):
            return pltpu.make_async_remote_copy(
                src_ref=buffer.at[slot], dst_ref=buffer.at[slot],
                send_sem=sems.at[0, k], recv_sem=sems.at[1, slot],
                device_id={"row": peer(k)}, device_id_type=MESH,
            )

        def start():
            @pl.loop(1, n)
            def _(k):
                copy(k, me).start()

        def finish():
            @pl.loop(1, n)
            def _(k):
                copy(k, peer(k)).wait_recv()

            @pl.loop(1, n)
            def _(k):
                copy(k, me).wait_send()

        return start, finish

    start_power, finish_power = exchange(powers, power_sem)
    start_ref, finish_ref = exchange(refs, ref_sem)
    start_power()

    def halo(t):
        up = pltpu.make_async_remote_copy(
            src_ref=x_ref.at[rows - t], dst_ref=low.at[HALF - t],
            send_sem=low_sem.at[0, t - 1], recv_sem=low_sem.at[1, t - 1],
            device_id={"row": jnp.minimum(me + 1, n - 1)}, device_id_type=MESH,
        )
        down = pltpu.make_async_remote_copy(
            src_ref=x_ref.at[t - 1], dst_ref=high.at[t - 1],
            send_sem=high_sem.at[0, t - 1], recv_sem=high_sem.at[1, t - 1],
            device_id={"row": jnp.maximum(me - 1, 0)}, device_id_type=MESH,
        )
        return up, down

    has_next = me < n - 1
    has_prev = me > 0
    for t in range(1, HALF + 1):
        up, down = halo(t)
        pl.when(has_next)(up.start)
        pl.when(has_prev)(down.start)

    @pl.when(me == 0)
    def _():
        low[...] = jnp.zeros_like(low)

    @pl.when(me == n - 1)
    def _():
        high[...] = jnp.zeros_like(high)

    row_ids = first_row + lax.broadcasted_iota(jnp.int32, (rows, cols), 0)
    col_ids = lax.broadcasted_iota(jnp.int32, (rows, cols), 1)
    chosen = []
    count = jnp.zeros((rows, cols), jnp.float32)
    for a in range(-HALF, HALF + 1):
        for b in range(-HALF, HALF + 1):
            inside = (row_ids + a >= 0) & (row_ids + a < total_rows)
            inside = inside & (col_ids + b >= 0) & (col_ids + b < cols)
            if (a, b) != (0, 0):
                inside = inside & (mask_ref[(a + HALF) * WIDTH + b + HALF] == 1)
            one = inside.astype(jnp.float32)
            chosen.append(one)
            count = count + one
    inverse = 1.0 / (count * ndate)

    def window(block):
        return max(0, block * LANE - SUB), min(cols, (block + 1) * LANE + SUB)

    coef[...] = jnp.zeros_like(coef)
    for block in range(blocks):
        begin, end = window(block)
        shape = (end - begin, LANE)
        shift = begin - block * LANE
        shift = shift + lax.broadcasted_iota(jnp.int32, shape, 0) - lax.broadcasted_iota(jnp.int32, shape, 1)
        for r in range(rows):
            for a in range(WIDTH):
                band = jnp.zeros(shape, jnp.float32)
                for b in range(WIDTH):
                    line = (chosen[a * WIDTH + b] * inverse)[r:r + 1, block * LANE:(block + 1) * LANE]
                    band = jnp.where(shift == b - HALF, line, band)
                weight[block, r, a, 0:end - begin, :] = band

    flat[depth:, :] = jnp.zeros((flat.shape[0] - depth, flat.shape[1]), flat.dtype)
    finish_power()
    power = jnp.sum(powers[...], axis=0)
    gain_row = lax.rsqrt(power * (1.0 / (total_rows * cols)) + 0.1)
    gain = jnp.broadcast_to(gain_row, (LANE, long_dates)).T[0:half_depth, :]
    gain = jnp.concatenate([gain] * blocks, axis=1)

    def calibrate(source, place):
        for part in range(2):
            rows_here = slice(part * half_depth, (part + 1) * half_depth)
            scaled = (source[rows_here, :].astype(jnp.float32) * gain).astype(jnp.bfloat16)
            flat[rows_here, place * cols:(place + 1) * cols] = scaled
        turned[place] = flat[:, place * cols:(place + 1) * cols].T

    def tile(r, block):
        start = (r + HALF) * cols + block * LANE
        return flat[0:half_depth, start:start + LANE], flat[half_depth:depth, start:start + LANE]

    def pair_of(real, imag):
        return jnp.concatenate(
            [jnp.concatenate([real, imag], axis=1), jnp.concatenate([imag, -real], axis=1)], axis=0
        )

    def project(r, block, a, pair):
        begin, end = window(block)
        proj = jnp.dot(turned[r + a, begin:end, 0:depth], pair, preferred_element_type=jnp.float32)
        band = weight[block, r, a, 0:end - begin, :]
        both = jnp.concatenate([band, band], axis=1)
        coef[block, a * cols + begin:a * cols + end, :] = (proj * both).astype(jnp.bfloat16)

    def update(r, block, first, last):
        return jnp.dot(
            flat[0:depth, (r + first) * cols:(r + last) * cols],
            coef[block, first * cols:last * cols, :], preferred_element_type=jnp.float32,
        )

    def partial_update(r, block, places):
        pair = pair_of(*tile(r, block))
        value = None
        for low_place, high_place in places:
            first, last = max(low_place - r, 0), min(high_place - r, WIDTH)
            if first >= last:
                continue
            for a in range(first, last):
                project(r, block, a, pair)
            term = update(r, block, first, last)
            value = term if value is None else value + term
        return value

    for r in range(rows):
        calibrate(x_ref.at[r], r + HALF)
    for r in range(rows):
        for block in range(blocks):
            total[r, block] = partial_update(r, block, [(HALF, HALF + rows)])

    def arrive(t):
        up, down = halo(t)
        pl.when(has_prev)(up.wait_recv)
        pl.when(has_next)(down.wait_recv)
        calibrate(low.at[HALF - t], HALF - t)
        calibrate(high.at[t - 1], HALF + rows + t - 1)

    def ring(t):
        return [(HALF - t, HALF - t + 1), (HALF + rows + t - 1, HALF + rows + t)]

    for t in range(1, HALF):
        arrive(t)
        for r in range(rows):
            for block in range(blocks):
                term = partial_update(r, block, ring(t))
                if term is not None:
                    total[r, block] += term
    arrive(HALF)

    target = index_ref[0]
    picked = jnp.zeros((depth, LANE), jnp.float32)
    for r in range(rows):
        for block in range(blocks):
            for step in range(ITERS):
                if step == 0:
                    product = total[r, block]
                    term = partial_update(r, block, ring(HALF))
                    if term is not None:
                        product = product + term
                else:
                    pair = pair_of(real, imag)
                    for a in range(WIDTH):
                        project(r, block, a, pair)
                    product = update(r, block, 0, WIDTH)
                top, bottom = product[0:half_depth], product[half_depth:depth]
                new_real = top[:, 0:LANE] - bottom[:, LANE:2 * LANE]
                new_imag = top[:, LANE:2 * LANE] + bottom[:, 0:LANE]
                energy = jnp.sum(new_real * new_real + new_imag * new_imag, axis=0, keepdims=True)
                factor = lax.rsqrt(energy * (1.0 / ndate) + 0.001)
                new_real = new_real * factor
                new_imag = new_imag * factor
                real = new_real.astype(jnp.bfloat16)
                imag = new_imag.astype(jnp.bfloat16)
            lanes = slice(block * LANE, (block + 1) * LANE)
            out_ref[r, 0:half_depth, lanes] = new_real
            out_ref[r, half_depth:depth, lanes] = new_imag
            place = (first_row + r) * cols + block * LANE + lax.broadcasted_iota(jnp.int32, (1, LANE), 1)
            here = place == target
            picked = picked + jnp.concatenate(
                [jnp.where(here, new_real, 0.0), jnp.where(here, new_imag, 0.0)], axis=0
            )

    column[...] = jnp.zeros_like(column)
    column[0:depth, :] = picked
    refs[me] = row_of(column[...])
    start_ref()
    finish_ref()
    refvec = jnp.sum(refs[...], axis=0)
    refvec = jnp.broadcast_to(refvec, (LANE, long_depth)).T
    ref_real = refvec[0:half_depth]
    ref_imag = refvec[half_depth:depth]
    for r in range(rows):
        for block in range(blocks):
            lanes = slice(block * LANE, (block + 1) * LANE)
            real = out_ref[r, 0:half_depth, lanes]
            imag = out_ref[r, half_depth:depth, lanes]
            out_ref[r, 0:half_depth, lanes] = real * ref_real + imag * ref_imag
            out_ref[r, half_depth:depth, lanes] = imag * ref_real - real * ref_imag

    for t in range(1, HALF + 1):
        up, down = halo(t)
        pl.when(has_next)(up.wait_send)
        pl.when(has_prev)(down.wait_send)


def per_device(slc, mask, ref_index):
    parts, ndate, rows, cols = slc.shape
    n = lax.axis_size("row")
    half_depth = round_up(ndate, SUB)
    depth = 2 * half_depth
    long_dates = round_up(half_depth, LANE)
    long_depth = round_up(depth, LANE)
    blocks = cols // LANE
    span = rows + 2 * HALF
    x = jnp.pad(slc.transpose(2, 0, 1, 3), ((0, 0), (0, 0), (0, half_depth - ndate), (0, 0)))
    x = x.reshape(rows, depth, cols)
    vmem = pl.BlockSpec(memory_space=pltpu.VMEM)

    def body(*refs):
        kernel(n, ndate, rows * n, *refs)

    out = pl.pallas_call(
        body,
        out_shape=jax.ShapeDtypeStruct((rows, depth, cols), jnp.float32),
        in_specs=[vmem, vmem, pl.BlockSpec(memory_space=pltpu.SMEM)],
        out_specs=vmem,
        scratch_shapes=[
            pltpu.VMEM((HALF, depth, cols), jnp.bfloat16),
            pltpu.VMEM((HALF, depth, cols), jnp.bfloat16),
            pltpu.VMEM((long_depth, span * cols), jnp.bfloat16),
            pltpu.VMEM((span, cols, long_depth), jnp.bfloat16),
            pltpu.VMEM((blocks, rows, WIDTH, LANE + 2 * SUB, LANE), jnp.float32),
            pltpu.VMEM((blocks, WIDTH * cols, 2 * LANE), jnp.bfloat16),
            pltpu.VMEM((rows, blocks, depth, 2 * LANE), jnp.float32),
            pltpu.VMEM((long_depth, LANE), jnp.float32),
            pltpu.VMEM((n, 1, long_dates), jnp.float32),
            pltpu.VMEM((n, 1, long_depth), jnp.float32),
            pltpu.SemaphoreType.DMA((2, HALF)),
            pltpu.SemaphoreType.DMA((2, HALF)),
            pltpu.SemaphoreType.DMA((2, n)),
            pltpu.SemaphoreType.DMA((2, n)),
        ],
        compiler_params=pltpu.CompilerParams(collective_id=0, has_side_effects=True),
        name="link",
    )(x, mask, ref_index)
    out = out.reshape(rows, parts, half_depth, cols)[:, :, :ndate]
    return out.transpose(1, 2, 0, 3)


def solution(mesh):
    placed = (P(None, None, ("grp", "row"), None), P(None, ("grp", "row"), None), P("grp"))
    return jax.shard_map(
        per_device,
        mesh=mesh,
        in_specs=placed,
        out_specs=P(None, None, ("grp", "row"), None),
        check_vma=False,
    )
```

profile of v0, /device:TPU:0, one launch (start us, length us, event | category | flops | bytes accessed | tf_op | source)
XLA Modules:
  0.0 40.0 jit_solution(14058616734155254170)
XLA Ops:
  0.7 1.2 %copy.7 = bf16[2,2,300,256]{3,2,1,0:T(8,128)(2,1)S(1)} copy(bf16[2,2,300,256]{3,0,2,1:T(2,128)(2,1)} %bitcast.9) | data formatting | bytes 1228800
  1.8 0.9 %pad.4.clone = bf16[2,2,304,256]{3,2,1,0:T(8,128)(2,1)} pad(bf16[2,2,300,256]{3,2,1,0:T(8,128)(2,1)S(1)} %copy.7, bf16[]{:T(256)} %constant.2.clone.1), padding=0_0x0_0x0_4x0_0 | pad | bytes 1236994 | tf_op jit(solution)/shard_map/jit(_pad)/pad | solution.py:286
  2.7 34.1 %link.1 = f32[2,608,256]{2,1,0:T(8,128)} custom-call(bf16[2,608,256]{2,1,0:T(8,128)(2,1)} %bitcast.8, s32[25,2,256]{2,1,0:T(2,128)} %refs_1_.1, s32[1]{0:T(128)S(6)} %copy.10.refs_2_), custom_call_target="tpu_custom_call" | custom-call | tf_op jit(solution)/shard_map/link/pallas_call | solution.py:293
  36.8 3.3 %copy.9 = f32[2,2,300,256]{3,0,2,1:T(2,128)} copy(f32[2,2,300,256]{3,2,1,0:T(8,128)} %bitcast.7) | data formatting | bytes 2457600
where the time goes:
time: 40.2 us; the launch traced here: 40 us
  Pallas kernels  34.1 us (85%)
  local copies, waits for them, and re-layouts  5.3 us (13%)
  between operations  0.66 us (2%)
    pallas_call x1, Pallas kernels, per_device(): pl.pallas_call(body, out_shape=jax.ShapeDtypeStruct((rows, depth, cols),...  34.1 us
    unnamed x2, local copies, waits for them, and re-layouts  4.43 us
    pad x1, local copies, waits for them, and re-layouts, per_device(): jnp.pad(slc.transpose(2, 0, 1, 3), ((0, 0), (0, 0), (0, half_depth - ndat...  0.87 us

commit v1 on v0

v1 whole, which is shorter than its diff:
```python
import jax
import jax.numpy as jnp
from jax import lax
from jax.experimental import pallas as pl
from jax.experimental.pallas import tpu as pltpu
from jax.sharding import PartitionSpec as P

HALF = 2
ITERS = 2
WIDTH = 2 * HALF + 1
LANE = 128
SUB = 16
MESH = pl.DeviceIdType.MESH


def round_up(value, unit):
    return (value + unit - 1) // unit * unit


def kernel(
    n, ndate, x_hbm, mask_ref, index_ref, out_ref,
    raw, wide, scene, turned, chosen, weight, pairs, coef, total, vectors, gains, column, powers, refs,
    load_sem, far_sem, near_sem, power_sem, ref_sem,
):
    _, rows, cols = mask_ref.shape
    span, blocks, depth, _ = scene.shape
    half = depth // 2
    long_depth = refs.shape[2]
    long_dates = powers.shape[2]
    total_rows = rows * n
    stride = blocks * rows
    me = lax.axis_index("row")
    odd = lax.rem(me, 2)
    near = me + 1 - 2 * odd
    far = me - 1 + 2 * odd
    has_near = near < n
    has_far = (far >= 0) & (far < n)
    first_row = me * rows

    def peer(k):
        return lax.rem(me + k, n)

    def place(q):
        return q + odd * (rows - 1 - 2 * q)

    load = pltpu.make_async_copy(x_hbm, raw, load_sem)
    load.start()
    barrier = pltpu.get_barrier_semaphore()

    @pl.loop(1, n)
    def _(k):
        pl.semaphore_signal(barrier, inc=1, device_id={"row": peer(k)}, device_id_type=MESH)

    row_ids = first_row + lax.broadcasted_iota(jnp.int32, (rows, cols), 0)
    col_ids = lax.broadcasted_iota(jnp.int32, (rows, cols), 1)
    count = jnp.zeros((rows, cols), jnp.float32)
    for a in range(WIDTH):
        step = a + odd * (WIDTH - 1 - 2 * a)
        for b in range(WIDTH):
            there = row_ids + (step - HALF)
            inside = (there >= 0) & (there < total_rows)
            inside = inside & (col_ids + (b - HALF) >= 0) & (col_ids + (b - HALF) < cols)
            if (a, b) != (HALF, HALF):
                inside = inside & (mask_ref[step * WIDTH + b] == 1)
            one = inside.astype(jnp.float32)
            chosen[a * WIDTH + b] = one
            count = count + one
    inverse = 1.0 / (count * ndate)
    for o in range(WIDTH * WIDTH):
        chosen[o] = chosen[o] * inverse

    def window(block):
        return max(0, block * LANE - SUB), min(cols, (block + 1) * LANE + SUB)

    coef[...] = jnp.zeros_like(coef)
    for block in range(blocks):
        begin, end = window(block)
        shape = (end - begin, LANE)
        shift = begin - block * LANE
        shift = shift + lax.broadcasted_iota(jnp.int32, shape, 0) - lax.broadcasted_iota(jnp.int32, shape, 1)
        for q in range(rows):
            for a in range(WIDTH):
                band = jnp.zeros(shape, jnp.float32)
                for b in range(WIDTH):
                    lanes = slice(block * LANE, (block + 1) * LANE)
                    line = chosen[a * WIDTH + b, q:q + 1, lanes]
                    line = jnp.where(odd == 1, chosen[a * WIDTH + b, rows - 1 - q:rows - q, lanes], line)
                    band = jnp.where(shift == b - HALF, line, band)
                weight[block, q, a, 0:end - begin, :] = band

    column[...] = jnp.zeros_like(column)

    load.wait()
    wide[0:raw.shape[0], :] = raw[...].astype(jnp.float32)
    sums = jnp.zeros((half, LANE), jnp.float32)
    dates = lax.broadcasted_iota(jnp.int32, (half, LANE), 0)
    for q in range(rows):
        for part in range(2):
            for block in range(blocks):
                start = part * ndate * stride + block * rows + place(q)
                piece = wide[pl.ds(start, half, stride=stride), :]
                piece = jnp.where(dates < ndate, piece, 0.0)
                scene[HALF + q, block, part * half:(part + 1) * half, :] = piece.astype(jnp.bfloat16)
                sums = sums + piece * piece
    column[0:half, :] = sums
    powers[me] = jnp.sum(column[0:long_dates, :].T, axis=0, keepdims=True)

    pl.semaphore_wait(barrier, n - 1)

    def exchange(buffer, sems):
        def copy(k, slot):
            return pltpu.make_async_remote_copy(
                src_ref=buffer.at[slot], dst_ref=buffer.at[slot],
                send_sem=sems.at[0, k], recv_sem=sems.at[1, slot],
                device_id={"row": peer(k)}, device_id_type=MESH,
            )

        def start():
            @pl.loop(1, n)
            def _(k):
                copy(k, me).start()

        def finish():
            @pl.loop(1, n)
            def _(k):
                copy(k, peer(k)).wait_recv()

            @pl.loop(1, n)
            def _(k):
                copy(k, me).wait_send()

        return start, finish

    start_power, finish_power = exchange(powers, power_sem)
    start_ref, finish_ref = exchange(refs, ref_sem)
    start_power()

    far_id = jnp.clip(far, 0, n - 1)
    near_id = jnp.clip(near, 0, n - 1)

    def far_copy(t):
        return pltpu.make_async_remote_copy(
            src_ref=scene.at[HALF + t], dst_ref=scene.at[HALF - 1 - t],
            send_sem=far_sem.at[0, t], recv_sem=far_sem.at[1, t],
            device_id={"row": far_id}, device_id_type=MESH,
        )

    def near_copy(t):
        return pltpu.make_async_remote_copy(
            src_ref=scene.at[HALF + rows - 1 - t], dst_ref=scene.at[HALF + rows + t],
            send_sem=near_sem.at[0, t], recv_sem=near_sem.at[1, t],
            device_id={"row": near_id}, device_id_type=MESH,
        )

    for t in range(HALF):
        pl.when(has_far)(far_copy(t).start)
    for t in range(HALF):
        pl.when(has_near)(near_copy(t).start)

    @pl.when(jnp.logical_not(has_far))
    def _():
        scene[0:HALF] = jnp.zeros((HALF, blocks, depth, LANE), scene.dtype)

    @pl.when(jnp.logical_not(has_near))
    def _():
        scene[HALF + rows:span] = jnp.zeros((HALF, blocks, depth, LANE), scene.dtype)

    def turn(slot):
        for block in range(blocks):
            tall = jnp.concatenate(
                [scene[slot, block], jnp.zeros((long_depth - depth, LANE), scene.dtype)], axis=0
            )
            turned[slot, block * LANE:(block + 1) * LANE, :] = tall.T

    for q in range(rows):
        turn(HALF + q)

    finish_power()
    power = jnp.sum(powers[...], axis=0)
    gain_row = lax.rsqrt(power * (1.0 / (total_rows * cols)) + 0.1)
    gains[...] = jnp.broadcast_to(gain_row, (LANE, long_dates)).T[0:half, :]

    def set_pair(q, block, real, imag):
        pairs[q, block, 0:half, 0:LANE] = real
        pairs[q, block, 0:half, LANE:2 * LANE] = imag
        pairs[q, block, half:depth, 0:LANE] = imag
        pairs[q, block, half:depth, LANE:2 * LANE] = -real

    for q in range(rows):
        for block in range(blocks):
            square = gains[...] * gains[...]
            tile = scene[HALF + q, block].astype(jnp.float32)
            set_pair(
                q, block, (tile[0:half] * square).astype(jnp.bfloat16), (tile[half:depth] * square).astype(jnp.bfloat16)
            )

    def project(q, block, slot):
        a = slot - q
        begin, end = window(block)
        proj = jnp.dot(turned[slot, begin:end, 0:depth], pairs[q, block], preferred_element_type=jnp.float32)
        band = weight[block, q, a, 0:end - begin, :]
        both = jnp.concatenate([band, band], axis=1)
        coef[q, block, a * cols + begin:a * cols + end, :] = (proj * both).astype(jnp.bfloat16)

    def update(q, block, slots):
        left = jnp.concatenate([scene[s, b] for s in slots for b in range(blocks)], axis=1)
        right = coef[q, block, (slots[0] - q) * cols:(slots[-1] + 1 - q) * cols, :]
        return jnp.dot(left, right, preferred_element_type=jnp.float32)

    def normalize(product):
        gain = gains[...]
        top, bottom = product[0:half], product[half:depth]
        real = (top[:, 0:LANE] - bottom[:, LANE:2 * LANE]) * gain
        imag = (top[:, LANE:2 * LANE] + bottom[:, 0:LANE]) * gain
        energy = jnp.sum(real * real + imag * imag, axis=0, keepdims=True)
        factor = lax.rsqrt(energy * (1.0 / ndate) + 0.001)
        return real * factor, imag * factor

    def rest(q, block, product):
        real, imag = normalize(product)
        for _ in range(1, ITERS):
            gain = gains[...]
            set_pair(q, block, (real * gain).astype(jnp.bfloat16), (imag * gain).astype(jnp.bfloat16))
            for slot in range(q, q + WIDTH):
                project(q, block, slot)
            real, imag = normalize(update(q, block, list(range(q, q + WIDTH))))
        vectors[q, block, 0:half, :] = real
        vectors[q, block, half:depth, :] = imag

    def seen(q, slots):
        return [s for s in slots if q <= s < q + WIDTH]

    for q in range(rows):
        for block in range(blocks):
            for slot in seen(q, range(HALF, HALF + rows)):
                project(q, block, slot)
    for t in range(HALF):
        pl.when(has_near)(near_copy(t).wait_recv)
        turn(HALF + rows + t)
    for q in range(rows):
        for block in range(blocks):
            for slot in seen(q, range(HALF + rows, span)):
                project(q, block, slot)

    def whole(q, block):
        rest(q, block, update(q, block, list(range(q, q + WIDTH))))

    for q in range(HALF, rows):
        for block in range(blocks):
            whole(q, block)
    for t in range(HALF):
        slot = HALF - 1 - t
        pl.when(has_far)(far_copy(t).wait_recv)
        turn(slot)
        for q in range(min(slot, rows - 1), -1, -1):
            for block in range(blocks):
                project(q, block, slot)
        for block in range(blocks):
            if slot > 0:
                if slot < rows:
                    whole(slot, block)
                if slot == 1:
                    total[0, block] = update(0, block, list(range(1, WIDTH)))
            else:
                rest(0, block, total[0, block] + update(0, block, [0]))

    target = index_ref[0]
    picked = jnp.zeros((depth, LANE), jnp.float32)
    for q in range(rows):
        for block in range(blocks):
            spot = (first_row + place(q)) * cols + block * LANE + lax.broadcasted_iota(jnp.int32, (1, LANE), 1)
            picked = picked + jnp.where(spot == target, vectors[q, block], 0.0)
    column[...] = jnp.zeros_like(column)
    column[0:depth, :] = picked
    refs[me] = jnp.sum(column[...].T, axis=0, keepdims=True)
    start_ref()
    finish_ref()
    refvec = jnp.sum(refs[...], axis=0)
    refvec = jnp.broadcast_to(refvec, (LANE, long_depth)).T
    ref_real = refvec[0:half]
    ref_imag = refvec[half:depth]
    for q in range(rows):
        for block in range(blocks):
            real = vectors[q, block, 0:half, :]
            imag = vectors[q, block, half:depth, :]
            start = block * rows + place(q)
            out_ref[pl.ds(start, ndate, stride=stride), :] = (real * ref_real + imag * ref_imag)[0:ndate]
            start = start + ndate * stride
            out_ref[pl.ds(start, ndate, stride=stride), :] = (imag * ref_real - real * ref_imag)[0:ndate]

    for t in range(HALF):
        pl.when(has_far)(far_copy(t).wait_send)
        pl.when(has_near)(near_copy(t).wait_send)


def per_device(slc, mask, ref_index):
    parts, ndate, rows, cols = slc.shape
    n = lax.axis_size("row")
    half = round_up(ndate, SUB)
    depth = 2 * half
    long_dates = round_up(half, LANE)
    long_depth = round_up(depth, LANE)
    blocks = cols // LANE
    span = rows + 2 * HALF
    lines = parts * ndate * blocks * rows
    x = slc.reshape(parts, ndate, rows, blocks, LANE).transpose(0, 1, 3, 2, 4).reshape(lines, LANE)
    vmem = pl.BlockSpec(memory_space=pltpu.VMEM)

    def body(*refs):
        kernel(n, ndate, *refs)

    out = pl.pallas_call(
        body,
        out_shape=jax.ShapeDtypeStruct((lines, LANE), jnp.float32),
        in_specs=[pl.BlockSpec(memory_space=pl.ANY), vmem, pl.BlockSpec(memory_space=pltpu.SMEM)],
        out_specs=vmem,
        scratch_shapes=[
            pltpu.VMEM((lines, LANE), jnp.bfloat16),
            pltpu.VMEM((lines + (half - ndate) * blocks * rows, LANE), jnp.float32),
            pltpu.VMEM((span, blocks, depth, LANE), jnp.bfloat16),
            pltpu.VMEM((span, cols, long_depth), jnp.bfloat16),
            pltpu.VMEM((WIDTH * WIDTH, rows, cols), jnp.float32),
            pltpu.VMEM((blocks, rows, WIDTH, LANE + 2 * SUB, LANE), jnp.float32),
            pltpu.VMEM((rows, blocks, depth, 2 * LANE), jnp.bfloat16),
            pltpu.VMEM((rows, blocks, WIDTH * cols, 2 * LANE), jnp.bfloat16),
            pltpu.VMEM((rows, blocks, depth, 2 * LANE), jnp.float32),
            pltpu.VMEM((rows, blocks, depth, LANE), jnp.float32),
            pltpu.VMEM((half, LANE), jnp.float32),
            pltpu.VMEM((long_depth, LANE), jnp.float32),
            pltpu.VMEM((n, 1, long_dates), jnp.float32),
            pltpu.VMEM((n, 1, long_depth), jnp.float32),
            pltpu.SemaphoreType.DMA,
            pltpu.SemaphoreType.DMA((2, HALF)),
            pltpu.SemaphoreType.DMA((2, HALF)),
            pltpu.SemaphoreType.DMA((2, n)),
            pltpu.SemaphoreType.DMA((2, n)),
        ],
        compiler_params=pltpu.CompilerParams(collective_id=0, has_side_effects=True),
        name="link",
    )(x, mask, ref_index)
    out = out.reshape(parts, ndate, blocks, rows, LANE).transpose(0, 1, 3, 2, 4)
    return out.reshape(parts, ndate, rows, cols)


def solution(mesh):
    placed = (P(None, None, ("grp", "row"), None), P(None, ("grp", "row"), None), P("grp"))
    return jax.shard_map(
        per_device,
        mesh=mesh,
        in_specs=placed,
        out_specs=P(None, None, ("grp", "row"), None),
        check_vma=False,
    )
```

time: 40.2 us -> 36.7 us (0.913)
  local copies, waits for them, and re-layouts: 5.3 us -> 2.74 us
  Pallas kernels: 34.1 us -> 33.1 us
    unnamed x2 -> x1, local copies, waits for them, and re-layouts: 4.43 us -> 2.74 us
    pallas_call x1, Pallas kernels: 34.1 us -> 33.1 us  [per_device(): pl.pallas_call(body, out_shape=jax.ShapeDtypeStruct((lines, LANE), jnp.fl...]
    pad x1 -> x0, local copies, waits for them, and re-layouts: 0.87 us -> none  [per_device(): jnp.pad(slc.transpose(2, 0, 1, 3), ((0, 0), (0, 0), (0, half_depth - ndat...]
where the time goes in v1:
time: 36.7 us; the launch traced here: 36.5 us
  Pallas kernels  33.1 us (90%)
  local copies, waits for them, and re-layouts  2.74 us (7%)
  between operations  0.66 us (2%)
    pallas_call x1, Pallas kernels, per_device(): pl.pallas_call(body, out_shape=jax.ShapeDtypeStruct((lines, LANE), jnp.fl...  33.1 us
    unnamed x1, local copies, waits for them, and re-layouts  2.74 us

profile of v1, /device:TPU:0, one launch (start us, length us, event | category | flops | bytes accessed | tf_op | source)
XLA Modules:
  0.0 36.5 jit_solution(16275565419479746855)
XLA Ops:
  0.7 33.1 %link.1 = f32[2400,128]{1,0:T(8,128)} custom-call(bf16[2400,128]{1,0:T(8,128)(2,1)} %bitcast.11, s32[25,2,256]{2,1,0:T(2,128)} %refs_1_.1, s32[1]{0:T(128)S(6)} %copy.7.refs_2_), custom_call_target="tpu_custom_call" | custom-call | tf_op jit(solution)/shard_map/link/pallas_call | solution.py:312
  33.7 2.7 %copy.8 = f32[2,300,2,256]{3,2,1,0:T(2,128)} copy(f32[2,300,2,256]{3,2,1,0:T(2,128)} %bitcast.10) | data formatting | bytes 2457600

commit v2 on v1

v2 whole, which is shorter than its diff:
```python
import jax
import jax.numpy as jnp
from jax import lax
from jax.experimental import pallas as pl
from jax.experimental.pallas import tpu as pltpu
from jax.sharding import PartitionSpec as P

HALF = 2
ITERS = 2
WIDTH = 2 * HALF + 1
LANE = 128
SUB = 16
VMEM_LIMIT = 32000000
MESH = pl.DeviceIdType.MESH


def round_up(value, unit):
    return (value + unit - 1) // unit * unit


def kernel(
    n, ndate, x_hbm, mask_hbm, index_ref, out_ref,
    raw, mask_ref, wide, scene, turned, chosen, picks, weight, pairs, coef, total, vectors, gains, long_gain, column, powers, refs,
    load_sem, mask_sem, far_sem, near_sem, power_sem, ref_sem,
):
    _, rows, cols = mask_ref.shape
    span, blocks, depth, _ = scene.shape
    half = depth // 2
    long_depth = refs.shape[3]
    long_dates = powers.shape[2]
    total_rows = rows * n
    stride = blocks * rows
    me = lax.axis_index("row")
    odd = lax.rem(me, 2)
    near = me + 1 - 2 * odd
    far = me - 1 + 2 * odd
    has_near = near < n
    has_far = (far >= 0) & (far < n)
    first_row = me * rows

    def peer(k):
        return lax.rem(me + k, n)

    def place(q):
        return q + odd * (rows - 1 - 2 * q)

    barrier = pltpu.get_barrier_semaphore()

    @pl.loop(1, n)
    def _(k):
        pl.semaphore_signal(barrier, inc=1, device_id={"row": peer(k)}, device_id_type=MESH)

    load = pltpu.make_async_copy(x_hbm, raw, load_sem)
    load.start()
    load_mask = pltpu.make_async_copy(mask_hbm, mask_ref, mask_sem)
    load_mask.start()
    column[...] = jnp.zeros_like(column)

    load.wait()
    wide[0:raw.shape[0], :] = raw[...].astype(jnp.float32)
    sums = jnp.zeros((half, LANE), jnp.float32)
    dates = lax.broadcasted_iota(jnp.int32, (half, LANE), 0)
    for q in range(rows):
        for part in range(2):
            for block in range(blocks):
                start = part * ndate * stride + block * rows + place(q)
                piece = wide[pl.ds(start, half, stride=stride), :]
                piece = jnp.where(dates < ndate, piece, 0.0)
                scene[HALF + q, block, part * half:(part + 1) * half, :] = piece.astype(jnp.bfloat16)
                sums = sums + piece * piece
    column[0:half, :] = sums
    powers[me] = jnp.sum(column[0:long_dates, :].T, axis=0, keepdims=True)

    pl.semaphore_wait(barrier, n - 1)

    def exchange(buffer, sems):
        def copy(k, slot):
            return pltpu.make_async_remote_copy(
                src_ref=buffer.at[slot], dst_ref=buffer.at[slot],
                send_sem=sems.at[0, k], recv_sem=sems.at[1, slot],
                device_id={"row": peer(k)}, device_id_type=MESH,
            )

        def start():
            @pl.loop(1, n)
            def _(k):
                copy(k, me).start()

        def finish():
            @pl.loop(1, n)
            def _(k):
                copy(k, peer(k)).wait_recv()

            @pl.loop(1, n)
            def _(k):
                copy(k, me).wait_send()

        return start, finish

    start_power, finish_power = exchange(powers, power_sem)
    start_power()

    far_id = jnp.clip(far, 0, n - 1)
    near_id = jnp.clip(near, 0, n - 1)

    def far_copy(t):
        return pltpu.make_async_remote_copy(
            src_ref=scene.at[HALF + t], dst_ref=scene.at[HALF - 1 - t],
            send_sem=far_sem.at[0, t], recv_sem=far_sem.at[1, t],
            device_id={"row": far_id}, device_id_type=MESH,
        )

    def near_copy(t):
        return pltpu.make_async_remote_copy(
            src_ref=scene.at[HALF + rows - 1 - t], dst_ref=scene.at[HALF + rows + t],
            send_sem=near_sem.at[0, t], recv_sem=near_sem.at[1, t],
            device_id={"row": near_id}, device_id_type=MESH,
        )

    for t in range(HALF):
        pl.when(has_far)(far_copy(t).start)
    for t in range(HALF):
        pl.when(has_near)(near_copy(t).start)

    @pl.when(jnp.logical_not(has_far))
    def _():
        scene[0:HALF] = jnp.zeros((HALF, blocks, depth, LANE), scene.dtype)

    @pl.when(jnp.logical_not(has_near))
    def _():
        scene[HALF + rows:span] = jnp.zeros((HALF, blocks, depth, LANE), scene.dtype)

    load_mask.wait()
    row_ids = first_row + lax.broadcasted_iota(jnp.int32, (rows, cols), 0)
    col_ids = lax.broadcasted_iota(jnp.int32, (rows, cols), 1)
    count = jnp.zeros((rows, cols), jnp.float32)
    ones = []
    for a in range(WIDTH):
        step = a + odd * (WIDTH - 1 - 2 * a)
        for b in range(WIDTH):
            there = row_ids + (step - HALF)
            inside = (there >= 0) & (there < total_rows)
            inside = inside & (col_ids + (b - HALF) >= 0) & (col_ids + (b - HALF) < cols)
            if (a, b) != (HALF, HALF):
                inside = inside & (mask_ref[step * WIDTH + b] == 1)
            one = inside.astype(jnp.float32)
            ones.append(one)
            count = count + one
    inverse = 1.0 / (count * ndate)
    for o in range(WIDTH * WIDTH):
        line = ones[o] * inverse
        for q in range(rows):
            chosen[q, o:o + 1, :] = jnp.where(odd == 1, line[rows - 1 - q:rows - q], line[q:q + 1])
    for q in range(rows):
        chosen[q, WIDTH * WIDTH:, :] = jnp.zeros((chosen.shape[1] - WIDTH * WIDTH, cols), jnp.float32)

    def window(block):
        return max(0, block * LANE - SUB), min(cols, (block + 1) * LANE + SUB)

    coef[...] = jnp.zeros_like(coef)
    for block in range(blocks):
        begin, end = window(block)
        shape = (end - begin, LANE)
        shift = begin - block * LANE
        shift = shift + lax.broadcasted_iota(jnp.int32, shape, 0) - lax.broadcasted_iota(jnp.int32, shape, 1)
        for q in range(rows):
            for a in range(WIDTH):
                band = jnp.zeros(shape, jnp.float32)
                for b in range(WIDTH):
                    line = chosen[q, a * WIDTH + b:a * WIDTH + b + 1, block * LANE:(block + 1) * LANE]
                    band = jnp.where(shift == b - HALF, line, band)
                weight[block, q, a, 0:end - begin, :] = band

    target = index_ref[0]
    target_row = lax.div(target, cols) - first_row
    target_col = lax.rem(target, cols)
    base = jnp.clip(lax.div(target_col + SUB - HALF, SUB) - 1, 0, cols // SUB - 2)
    home = lax.broadcasted_iota(jnp.int32, (1, long_depth), 1) * 0 + target_row

    def turn(slot):
        for block in range(blocks):
            tall = jnp.concatenate(
                [scene[slot, block], jnp.zeros((long_depth - depth, LANE), scene.dtype)], axis=0
            )
            turned[slot, block * LANE:(block + 1) * LANE, :] = tall.T
        first = jnp.zeros((SUB, long_depth), scene.dtype)
        second = first
        group = lax.broadcasted_iota(jnp.int32, (SUB, long_depth), 1) * 0 + base
        for k in range(cols // SUB):
            piece = turned[slot, k * SUB:(k + 1) * SUB, :]
            first = first + piece * (group == k).astype(jnp.float32).astype(scene.dtype)
            second = second + piece * (group == k - 1).astype(jnp.float32).astype(scene.dtype)
        picks[slot, 0:SUB, :] = first
        picks[slot, SUB:2 * SUB, :] = second

    for q in range(rows):
        turn(HALF + q)

    finish_power()
    power = jnp.sum(powers[...], axis=0)
    gain_row = lax.rsqrt(power * (1.0 / (total_rows * cols)) + 0.1)
    gains[...] = jnp.broadcast_to(gain_row, (LANE, long_dates)).T[0:half, :]
    tall = jnp.concatenate([gains[...], gains[...], jnp.zeros((long_depth - depth, LANE), jnp.float32)], axis=0)
    long_gain[...] = tall.T[0:8, :]

    def set_pair(q, block, real, imag):
        pairs[q, block, 0:half, 0:LANE] = real
        pairs[q, block, 0:half, LANE:2 * LANE] = imag
        pairs[q, block, half:depth, 0:LANE] = imag
        pairs[q, block, half:depth, LANE:2 * LANE] = -real

    for q in range(rows):
        for block in range(blocks):
            square = gains[...] * gains[...]
            tile = scene[HALF + q, block].astype(jnp.float32)
            set_pair(
                q, block, (tile[0:half] * square).astype(jnp.bfloat16), (tile[half:depth] * square).astype(jnp.bfloat16)
            )

    def project(q, block, slots):
        begin, end = window(block)
        size = end - begin
        left = jnp.concatenate([turned[slot, begin:end, 0:depth] for slot in slots], axis=0)
        proj = jnp.dot(left, pairs[q, block], preferred_element_type=jnp.float32)
        for i, slot in enumerate(slots):
            a = slot - q
            band = weight[block, q, a, 0:size, :]
            both = jnp.concatenate([band, band], axis=1)
            part = proj[i * size:(i + 1) * size] * both
            coef[q, block, a * cols + begin:a * cols + end, :] = part.astype(jnp.bfloat16)

    def update(q, block, slots):
        left = jnp.concatenate([scene[s, b] for s in slots for b in range(blocks)], axis=1)
        right = coef[q, block, (slots[0] - q) * cols:(slots[-1] + 1 - q) * cols, :]
        return jnp.dot(left, right, preferred_element_type=jnp.float32)

    def normalize(product):
        gain = gains[...]
        top, bottom = product[0:half], product[half:depth]
        real = (top[:, 0:LANE] - bottom[:, LANE:2 * LANE]) * gain
        imag = (top[:, LANE:2 * LANE] + bottom[:, 0:LANE]) * gain
        energy = jnp.sum(real * real + imag * imag, axis=0, keepdims=True)
        factor = lax.rsqrt(energy * (1.0 / ndate) + 0.001)
        return real * factor, imag * factor

    def rest(q, block, product):
        real, imag = normalize(product)
        for _ in range(1, ITERS):
            gain = gains[...]
            set_pair(q, block, (real * gain).astype(jnp.bfloat16), (imag * gain).astype(jnp.bfloat16))
            project(q, block, list(range(q, q + WIDTH)))
            real, imag = normalize(update(q, block, list(range(q, q + WIDTH))))
        vectors[q, block, 0:half, :] = real
        vectors[q, block, half:depth, :] = imag

    def seen(q, slots):
        return [s for s in slots if q <= s < q + WIDTH]

    for t in range(HALF):
        pl.when(has_near)(near_copy(t).wait_recv)
        turn(HALF + rows + t)
    for q in range(rows):
        for block in range(blocks):
            project(q, block, seen(q, range(HALF, span)))

    def whole(q, block):
        rest(q, block, update(q, block, list(range(q, q + WIDTH))))

    def swap(x):
        lanes = lax.broadcasted_iota(jnp.int32, x.shape, 1)
        ahead = pltpu.roll(x, long_depth - half, 1)
        behind = pltpu.roll(x, half, 1)
        return jnp.where(lanes < half, -ahead, jnp.where(lanes < depth, behind, 0.0))

    def reference_vector(q):
        shape = (2 * SUB, WIDTH * 2 * SUB)
        offset = lax.broadcasted_iota(jnp.int32, shape, 0)
        line = lax.broadcasted_iota(jnp.int32, shape, 1)
        hit = line - (offset // WIDTH) * (2 * SUB) == target_col - HALF - base * SUB + offset % WIDTH
        hit = hit & (line // (2 * SUB) == offset // WIDTH)
        left = hit.astype(jnp.float32).astype(jnp.bfloat16)
        right = jnp.concatenate([picks[q + a] for a in range(WIDTH)], axis=0)
        stack = jnp.dot(left, right, preferred_element_type=jnp.float32)
        lanes = lax.broadcasted_iota(jnp.int32, (2 * SUB, cols), 1)
        bands = jnp.sum(jnp.where(lanes == target_col, chosen[q], 0.0), axis=1, keepdims=True)
        middle = HALF * WIDTH + HALF
        center = stack[middle:middle + 1]
        gain = long_gain[0:1, :]
        vector = center * gain
        for _ in range(ITERS):
            vector = vector * gain
            proj_real = jnp.sum(stack * vector, axis=1, keepdims=True) * bands
            proj_imag = jnp.sum(stack * -swap(vector), axis=1, keepdims=True) * bands
            vector = jnp.sum(stack * proj_real, axis=0, keepdims=True)
            vector = vector + swap(jnp.sum(stack * proj_imag, axis=0, keepdims=True))
            vector = vector * gain
            energy = jnp.sum(vector * vector, axis=1, keepdims=True)
            vector = vector * lax.rsqrt(energy * (1.0 / ndate) + 0.001)
        return vector

    finish = []

    def send_reference(q):
        refs[q, me] = jnp.where(home == place(q), reference_vector(q), 0.0)
        start, end = exchange(refs.at[q], ref_sem.at[q])
        start()
        finish.append(end)

    for q in range(HALF, rows):
        send_reference(q)
        for block in range(blocks):
            whole(q, block)
    for t in range(HALF):
        slot = HALF - 1 - t
        pl.when(has_far)(far_copy(t).wait_recv)
        turn(slot)
        if slot < rows:
            send_reference(slot)
        for q in range(min(slot, rows - 1), -1, -1):
            for block in range(blocks):
                project(q, block, [slot])
        for block in range(blocks):
            if slot > 0:
                if slot < rows:
                    whole(slot, block)
                if slot == 1:
                    total[0, block] = update(0, block, list(range(1, WIDTH)))
            else:
                rest(0, block, total[0, block] + update(0, block, [0]))

    for end in finish:
        end()
    refvec = jnp.sum(jnp.sum(refs[...], axis=0), axis=0)
    refvec = jnp.broadcast_to(refvec, (LANE, long_depth)).T
    ref_real = refvec[0:half]
    ref_imag = refvec[half:depth]
    for q in range(rows):
        for block in range(blocks):
            real = vectors[q, block, 0:half, :]
            imag = vectors[q, block, half:depth, :]
            start = block * rows + place(q)
            out_ref[pl.ds(start, ndate, stride=stride), :] = (real * ref_real + imag * ref_imag)[0:ndate]
            start = start + ndate * stride
            out_ref[pl.ds(start, ndate, stride=stride), :] = (imag * ref_real - real * ref_imag)[0:ndate]

    for t in range(HALF):
        pl.when(has_far)(far_copy(t).wait_send)
        pl.when(has_near)(near_copy(t).wait_send)


def per_device(slc, mask, ref_index):
    parts, ndate, rows, cols = slc.shape
    n = lax.axis_size("row")
    half = round_up(ndate, SUB)
    depth = 2 * half
    long_dates = round_up(half, LANE)
    long_depth = round_up(depth, LANE)
    blocks = cols // LANE
    span = rows + 2 * HALF
    lines = parts * ndate * blocks * rows
    x = slc.reshape(parts, ndate, rows, blocks, LANE).transpose(0, 1, 3, 2, 4).reshape(lines, LANE)
    vmem = pl.BlockSpec(memory_space=pltpu.VMEM)
    anywhere = pl.BlockSpec(memory_space=pltpu.HBM)

    def body(*refs):
        kernel(n, ndate, *refs)

    out = pl.pallas_call(
        body,
        out_shape=jax.ShapeDtypeStruct((lines, LANE), jnp.float32),
        in_specs=[anywhere, anywhere, pl.BlockSpec(memory_space=pltpu.SMEM)],
        out_specs=vmem,
        scratch_shapes=[
            pltpu.VMEM((lines, LANE), jnp.bfloat16),
            pltpu.VMEM(mask.shape, jnp.int32),
            pltpu.VMEM((lines + (half - ndate) * blocks * rows, LANE), jnp.float32),
            pltpu.VMEM((span, blocks, depth, LANE), jnp.bfloat16),
            pltpu.VMEM((span, cols, long_depth), jnp.bfloat16),
            pltpu.VMEM((rows, 2 * SUB, cols), jnp.float32),
            pltpu.VMEM((span, 2 * SUB, long_depth), jnp.bfloat16),
            pltpu.VMEM((blocks, rows, WIDTH, LANE + 2 * SUB, LANE), jnp.float32),
            pltpu.VMEM((rows, blocks, depth, 2 * LANE), jnp.bfloat16),
            pltpu.VMEM((rows, blocks, WIDTH * cols, 2 * LANE), jnp.bfloat16),
            pltpu.VMEM((rows, blocks, depth, 2 * LANE), jnp.float32),
            pltpu.VMEM((rows, blocks, depth, LANE), jnp.float32),
            pltpu.VMEM((half, LANE), jnp.float32),
            pltpu.VMEM((8, long_depth), jnp.float32),
            pltpu.VMEM((long_depth, LANE), jnp.float32),
            pltpu.VMEM((n, 1, long_dates), jnp.float32),
            pltpu.VMEM((rows, n, 1, long_depth), jnp.float32),
            pltpu.SemaphoreType.DMA,
            pltpu.SemaphoreType.DMA,
            pltpu.SemaphoreType.DMA((2, HALF)),
            pltpu.SemaphoreType.DMA((2, HALF)),
            pltpu.SemaphoreType.DMA((2, n)),
            pltpu.SemaphoreType.DMA((rows, 2, n)),
        ],
        compiler_params=pltpu.CompilerParams(collective_id=0, has_side_effects=True, vmem_limit_bytes=VMEM_LIMIT),
        name="link",
    )(pltpu.with_memory_space_constraint(x, pltpu.HBM), pltpu.with_memory_space_constraint(mask, pltpu.HBM), ref_index)

    def put(in_ref, out_ref, sem):
        copy = pltpu.make_async_copy(in_ref, out_ref, sem)
        copy.start()
        copy.wait()

    out = pl.pallas_call(
        put,
        out_shape=jax.ShapeDtypeStruct((lines, LANE), jnp.float32),
        in_specs=[vmem],
        out_specs=anywhere,
        scratch_shapes=[pltpu.SemaphoreType.DMA],
        compiler_params=pltpu.CompilerParams(vmem_limit_bytes=16 * 1024 * 1024),
        name="put",
    )(out)
    out = out.reshape(parts, ndate, blocks, rows, LANE).transpose(0, 1, 3, 2, 4)
    return out.reshape(parts, ndate, rows, cols)


def solution(mesh):
    placed = (P(None, None, ("grp", "row"), None), P(None, ("grp", "row"), None), P("grp"))
    return jax.shard_map(
        per_device,
        mesh=mesh,
        in_specs=placed,
        out_specs=P(None, None, ("grp", "row"), None),
        check_vma=False,
    )
```

time: 36.7 us -> 31.8 us (0.87)
  local copies, waits for them, and re-layouts: 2.74 us -> 0 us
  Pallas kernels: 33.1 us -> 31 us
    pallas_call x1, Pallas kernels: 33.1 us -> 30 us  [per_device(): pl.pallas_call(body, out_shape=jax.ShapeDtypeStruct((lines, LANE), jnp.fl...]
    unnamed x1 -> x0, local copies, waits for them, and re-layouts: 2.74 us -> none
    pallas_call x0 -> x1, Pallas kernels: none -> 1.04 us  [per_device(): pl.pallas_call(put, out_shape=jax.ShapeDtypeStruct((lines, LANE), jnp.flo...]
where the time goes in v2:
time: 31.8 us; the launch traced here: 31.7 us
  Pallas kernels  31 us (97%)
  between operations  0.66 us (2%)
    pallas_call x1, Pallas kernels, per_device(): pl.pallas_call(body, out_shape=jax.ShapeDtypeStruct((lines, LANE), jnp.fl...  30 us
    pallas_call x1, Pallas kernels, per_device(): pl.pallas_call(put, out_shape=jax.ShapeDtypeStruct((lines, LANE), jnp.flo...  1.04 us

profile of v2, /device:TPU:0, one launch (start us, length us, event | category | flops | bytes accessed | tf_op | source)
XLA Modules:
  0.0 31.7 jit_solution(13079397685013238746)
XLA Ops:
  0.7 30.0 %link.1.in_ref = f32[2400,128]{1,0:T(8,128)S(1)} custom-call(bf16[2400,128]{1,0:T(8,128)(2,1)} %bitcast.10, s32[25,2,256]{2,1,0:T(2,128)} %refs_1_.1, s32[1]{0:T(128)S(6)} %copy.6.refs_2_), custom_call_target="tpu_custom_call" | custom-call | tf_op jit(solution)/shard_map/link/pallas_call | solution.py:368
  30.6 1.0 %put.1 = f32[2400,128]{1,0:T(8,128)} custom-call(f32[2400,128]{1,0:T(8,128)S(1)} %link.1.in_ref), custom_call_target="tpu_custom_call" | custom-call | tf_op jit(solution)/shard_map/put/pallas_call | solution.py:407

commit v3 on v2

--- a/solution.py
+++ b/solution.py
@@ -20,12 +20,13 @@
 
 def kernel(
     n, ndate, x_hbm, mask_hbm, index_ref, out_ref,
-    raw, mask_ref, wide, scene, turned, chosen, picks, weight, pairs, coef, total, vectors, gains, long_gain, column, powers, refs,
+    raw, mask_ref, wide, scene, turned, chosen, picks, weight, pairs, coef, late, edges, total, vectors, gains, long_gain, column, powers, refs,
     load_sem, mask_sem, far_sem, near_sem, power_sem, ref_sem,
 ):
     _, rows, cols = mask_ref.shape
     span, blocks, depth, _ = scene.shape
     half = depth // 2
+    tiles = turned.shape[1]
     long_depth = refs.shape[3]
     long_dates = powers.shape[2]
     total_rows = rows * n
@@ -82,8 +83,7 @@
             )
 
         def start():
-            @pl.loop(1, n)
-            def _(k):
+            for k in range(1, n):
                 copy(k, me).start()
 
         def finish():
@@ -158,6 +158,7 @@
         return max(0, block * LANE - SUB), min(cols, (block + 1) * LANE + SUB)
 
     coef[...] = jnp.zeros_like(coef)
+    late[...] = jnp.zeros_like(late)
     for block in range(blocks):
         begin, end = window(block)
         shape = (end - begin, LANE)
@@ -179,19 +180,46 @@
 
     def turn(slot):
         for block in range(blocks):
-            tall = jnp.concatenate(
-                [scene[slot, block], jnp.zeros((long_depth - depth, LANE), scene.dtype)], axis=0
-            )
-            turned[slot, block * LANE:(block + 1) * LANE, :] = tall.T
-        first = jnp.zeros((SUB, long_depth), scene.dtype)
-        second = first
-        group = lax.broadcasted_iota(jnp.int32, (SUB, long_depth), 1) * 0 + base
-        for k in range(cols // SUB):
-            piece = turned[slot, k * SUB:(k + 1) * SUB, :]
-            first = first + piece * (group == k).astype(jnp.float32).astype(scene.dtype)
-            second = second + piece * (group == k - 1).astype(jnp.float32).astype(scene.dtype)
-        picks[slot, 0:SUB, :] = first
-        picks[slot, SUB:2 * SUB, :] = second
+            lines = slice(block * LANE, (block + 1) * LANE)
+            for i in range(tiles):
+                deep = slice(i * LANE, min((i + 1) * LANE, depth))
+                tile = scene[slot, block, deep, :]
+                if tile.shape[0] < LANE:
+                    tile = jnp.concatenate([tile, jnp.zeros((LANE - tile.shape[0], LANE), tile.dtype)], axis=0)
+                turned[slot, i, lines, :] = tile.T
+        group = lax.broadcasted_iota(jnp.int32, (SUB, LANE), 1) * 0 + base
+        hits = [(group == k).astype(jnp.float32).astype(scene.dtype) for k in range(-1, cols // SUB)]
+        for i in range(tiles):
+            first = jnp.zeros((SUB, LANE), scene.dtype)
+            second = first
+            for k in range(cols // SUB):
+                piece = turned[slot, i, k * SUB:(k + 1) * SUB, :]
+                first = first + piece * hits[k + 1]
+                second = second + piece * hits[k]
+            picks[slot, i, 0:SUB, :] = first
+            picks[slot, i, SUB:2 * SUB, :] = second
+
+    def sides(block):
+        ends = []
+        if block > 0:
+            ends.append(block * LANE - SUB)
+        if block < blocks - 1:
+            ends.append((block + 1) * LANE)
+        return ends
+
+    def set_edges(low):
+        for block in range(blocks):
+            for i in range(tiles):
+                parts = []
+                for end in sides(block):
+                    if low > 0:
+                        parts.append(jnp.zeros((low * SUB, LANE), edges.dtype))
+                    for slot in range(low, span):
+                        parts.append(turned[slot, i, end:end + SUB, :])
+                used = len(sides(block)) * span * SUB
+                if used < edges.shape[2]:
+                    parts.append(jnp.zeros((edges.shape[2] - used, LANE), edges.dtype))
+                edges[block, i * LANE:(i + 1) * LANE, :] = jnp.concatenate(parts, axis=0).T
 
     for q in range(rows):
         turn(HALF + q)
@@ -204,10 +232,10 @@
     long_gain[...] = tall.T[0:8, :]
 
     def set_pair(q, block, real, imag):
-        pairs[q, block, 0:half, 0:LANE] = real
-        pairs[q, block, 0:half, LANE:2 * LANE] = imag
-        pairs[q, block, half:depth, 0:LANE] = imag
-        pairs[q, block, half:depth, LANE:2 * LANE] = -real
+        pairs[q, block, 0, 0:half, :] = real
+        pairs[q, block, 1, 0:half, :] = imag
+        pairs[q, block, 0, half:depth, :] = imag
+        pairs[q, block, 1, half:depth, :] = -real
 
     for q in range(rows):
         for block in range(blocks):
@@ -217,21 +245,37 @@
                 q, block, (tile[0:half] * square).astype(jnp.bfloat16), (tile[half:depth] * square).astype(jnp.bfloat16)
             )
 
-    def project(q, block, slots):
+    def project(q, block, slots, into_late=False):
         begin, end = window(block)
         size = end - begin
-        left = jnp.concatenate([turned[slot, begin:end, 0:depth] for slot in slots], axis=0)
-        proj = jnp.dot(left, pairs[q, block], preferred_element_type=jnp.float32)
+        main = block * LANE - begin
+        left = jnp.concatenate(
+            [jnp.concatenate([turned[slot, i, begin:end, :] for i in range(tiles)], axis=1) for slot in slots], axis=0
+        )
+        right = jnp.concatenate([pairs[q, block, 0], pairs[q, block, 1]], axis=1)
+        proj = jnp.dot(left[:, 0:depth], right, preferred_element_type=jnp.float32)
         for i, slot in enumerate(slots):
             a = slot - q
             band = weight[block, q, a, 0:size, :]
-            both = jnp.concatenate([band, band], axis=1)
-            part = proj[i * size:(i + 1) * size] * both
-            coef[q, block, a * cols + begin:a * cols + end, :] = part.astype(jnp.bfloat16)
+            for c in range(2):
+                part = (proj[i * size:(i + 1) * size, c * LANE:(c + 1) * LANE] * band).astype(jnp.bfloat16)
+                if into_late:
+                    late[q, block, c, begin:end, :] = part
+                    continue
+                coef[q, block, c, a * LANE:(a + 1) * LANE, :] = part[main:main + LANE]
+                for k, side in enumerate(sides(block)):
+                    spot = WIDTH * LANE + (k * span + slot) * SUB
+                    coef[q, block, c, spot:spot + SUB, :] = part[side - begin:side - begin + SUB]
 
     def update(q, block, slots):
-        left = jnp.concatenate([scene[s, b] for s in slots for b in range(blocks)], axis=1)
-        right = coef[q, block, (slots[0] - q) * cols:(slots[-1] + 1 - q) * cols, :]
+        left = jnp.concatenate([scene[s, block] for s in slots] + [edges[block, 0:depth, :]], axis=1)
+        first = (slots[0] - q) * LANE
+        right = jnp.concatenate([coef[q, block, 0, first:, :], coef[q, block, 1, first:, :]], axis=1)
+        return jnp.dot(left, right, preferred_element_type=jnp.float32)
+
+    def late_update(q, block, slot):
+        left = jnp.concatenate([scene[slot, b] for b in range(blocks)], axis=1)
+        right = jnp.concatenate([late[q, block, 0], late[q, block, 1]], axis=1)
         return jnp.dot(left, right, preferred_element_type=jnp.float32)
 
     def normalize(product):
@@ -243,15 +287,25 @@
         factor = lax.rsqrt(energy * (1.0 / ndate) + 0.001)
         return real * factor, imag * factor
 
-    def rest(q, block, product):
+    def first_step(q, block, product):
         real, imag = normalize(product)
-        for _ in range(1, ITERS):
-            gain = gains[...]
-            set_pair(q, block, (real * gain).astype(jnp.bfloat16), (imag * gain).astype(jnp.bfloat16))
-            project(q, block, list(range(q, q + WIDTH)))
-            real, imag = normalize(update(q, block, list(range(q, q + WIDTH))))
-        vectors[q, block, 0:half, :] = real
-        vectors[q, block, half:depth, :] = imag
+        gain = gains[...]
+        set_pair(q, block, (real * gain).astype(jnp.bfloat16), (imag * gain).astype(jnp.bfloat16))
+
+    def last_steps(q):
+        window_slots = list(range(q, q + WIDTH))
+        for i in range(1, ITERS):
+            for block in range(blocks):
+                project(q, block, window_slots)
+            products = [update(q, block, window_slots) for block in range(blocks)]
+            for block in range(blocks):
+                real, imag = normalize(products[block])
+                if i < ITERS - 1:
+                    gain = gains[...]
+                    set_pair(q, block, (real * gain).astype(jnp.bfloat16), (imag * gain).astype(jnp.bfloat16))
+                else:
+                    vectors[q, block, 0:half, :] = real
+                    vectors[q, block, half:depth, :] = imag
 
     def seen(q, slots):
         return [s for s in slots if q <= s < q + WIDTH]
@@ -259,12 +313,13 @@
     for t in range(HALF):
         pl.when(has_near)(near_copy(t).wait_recv)
         turn(HALF + rows + t)
-    for q in range(rows):
-        for block in range(blocks):
-            project(q, block, seen(q, range(HALF, span)))
-
-    def whole(q, block):
-        rest(q, block, update(q, block, list(range(q, q + WIDTH))))
+    set_edges(HALF)
+    for q in range(rows):
+        slots = seen(q, range(HALF, span))
+        for block in range(blocks):
+            project(q, block, slots)
+        for block in range(blocks):
+            total[q, block] = update(q, block, slots)
 
     def swap(x):
         lanes = lax.broadcasted_iota(jnp.int32, x.shape, 1)
@@ -279,7 +334,9 @@
         hit = line - (offset // WIDTH) * (2 * SUB) == target_col - HALF - base * SUB + offset % WIDTH
         hit = hit & (line // (2 * SUB) == offset // WIDTH)
         left = hit.astype(jnp.float32).astype(jnp.bfloat16)
-        right = jnp.concatenate([picks[q + a] for a in range(WIDTH)], axis=0)
+        right = jnp.concatenate(
+            [jnp.concatenate([picks[q + a, i] for i in range(tiles)], axis=1) for a in range(WIDTH)], axis=0
+        )
         stack = jnp.dot(left, right, preferred_element_type=jnp.float32)
         lanes = lax.broadcasted_iota(jnp.int32, (2 * SUB, cols), 1)
         bands = jnp.sum(jnp.where(lanes == target_col, chosen[q], 0.0), axis=1, keepdims=True)
@@ -300,33 +357,39 @@
 
     finish = []
 
+    def set_reference(q):
+        refs[q, me] = jnp.where(home == place(q), reference_vector(q), 0.0)
+
     def send_reference(q):
-        refs[q, me] = jnp.where(home == place(q), reference_vector(q), 0.0)
         start, end = exchange(refs.at[q], ref_sem.at[q])
         start()
         finish.append(end)
 
     for q in range(HALF, rows):
+        set_reference(q)
         send_reference(q)
         for block in range(blocks):
-            whole(q, block)
+            first_step(q, block, total[q, block])
+        last_steps(q)
     for t in range(HALF):
         slot = HALF - 1 - t
         pl.when(has_far)(far_copy(t).wait_recv)
         turn(slot)
+        set_edges(slot)
         if slot < rows:
+            set_reference(slot)
+        for q in range(min(slot, rows - 1), -1, -1):
+            for block in range(blocks):
+                project(q, block, [slot], into_late=True)
+        if slot < rows:
+            products = [late_update(slot, block, slot) for block in range(blocks)]
+            for block in range(blocks):
+                first_step(slot, block, total[slot, block] + products[block])
             send_reference(slot)
-        for q in range(min(slot, rows - 1), -1, -1):
-            for block in range(blocks):
-                project(q, block, [slot])
-        for block in range(blocks):
-            if slot > 0:
-                if slot < rows:
-                    whole(slot, block)
-                if slot == 1:
-                    total[0, block] = update(0, block, list(range(1, WIDTH)))
-            else:
-                rest(0, block, total[0, block] + update(0, block, [0]))
+            last_steps(slot)
+        for q in range(min(slot, rows) - 1, -1, -1):
+            for block in range(blocks):
+                total[q, block] += late_update(q, block, slot)
 
     for end in finish:
         end()
@@ -358,6 +421,7 @@
     blocks = cols // LANE
     span = rows + 2 * HALF
     lines = parts * ndate * blocks * rows
+    margin = round_up(min(2, blocks - 1) * span * SUB, LANE)
     x = slc.reshape(parts, ndate, rows, blocks, LANE).transpose(0, 1, 3, 2, 4).reshape(lines, LANE)
     vmem = pl.BlockSpec(memory_space=pltpu.VMEM)
     anywhere = pl.BlockSpec(memory_space=pltpu.HBM)
@@ -375,12 +439,14 @@
             pltpu.VMEM(mask.shape, jnp.int32),
             pltpu.VMEM((lines + (half - ndate) * blocks * rows, LANE), jnp.float32),
             pltpu.VMEM((span, blocks, depth, LANE), jnp.bfloat16),
-            pltpu.VMEM((span, cols, long_depth), jnp.bfloat16),
+            pltpu.VMEM((span, long_depth // LANE, cols, LANE), jnp.bfloat16),
             pltpu.VMEM((rows, 2 * SUB, cols), jnp.float32),
-            pltpu.VMEM((span, 2 * SUB, long_depth), jnp.bfloat16),
+            pltpu.VMEM((span, long_depth // LANE, 2 * SUB, LANE), jnp.bfloat16),
             pltpu.VMEM((blocks, rows, WIDTH, LANE + 2 * SUB, LANE), jnp.float32),
-            pltpu.VMEM((rows, blocks, depth, 2 * LANE), jnp.bfloat16),
-            pltpu.VMEM((rows, blocks, WIDTH * cols, 2 * LANE), jnp.bfloat16),
+            pltpu.VMEM((rows, blocks, 2, depth, LANE), jnp.bfloat16),
+            pltpu.VMEM((rows, blocks, 2, WIDTH * LANE + margin, LANE), jnp.bfloat16),
+            pltpu.VMEM((rows, blocks, 2, cols, LANE), jnp.bfloat16),
+            pltpu.VMEM((blocks, long_depth, margin), jnp.bfloat16),
             pltpu.VMEM((rows, blocks, depth, 2 * LANE), jnp.float32),
             pltpu.VMEM((rows, blocks, depth, LANE), jnp.float32),
             pltpu.VMEM((half, LANE), jnp.float32),

time: 31.8 us -> 29.5 us (0.928)
  Pallas kernels: 31 us -> 28.7 us
    pallas_call x1, Pallas kernels: 30 us -> 27.7 us  [per_device(): pl.pallas_call(body, out_shape=jax.ShapeDtypeStruct((lines, LANE), jnp.fl...]
where the time goes in v3:
time: 29.5 us; the launch traced here: 29.4 us
  Pallas kernels  28.7 us (97%)
  between operations  0.66 us (2%)
    pallas_call x1, Pallas kernels, per_device(): pl.pallas_call(body, out_shape=jax.ShapeDtypeStruct((lines, LANE), jnp.fl...  27.7 us
    pallas_call x1, Pallas kernels, per_device(): pl.pallas_call(put, out_shape=jax.ShapeDtypeStruct((lines, LANE), jnp.flo...  1.04 us

profile of v3, /device:TPU:0, one launch (start us, length us, event | category | flops | bytes accessed | tf_op | source)
XLA Modules:
  0.0 29.4 jit_solution(12745595996545533206)
XLA Ops:
  0.7 27.7 %link.1.in_ref = f32[2400,128]{1,0:T(8,128)S(1)} custom-call(bf16[2400,128]{1,0:T(8,128)(2,1)} %bitcast.10, s32[25,2,256]{2,1,0:T(2,128)} %refs_1_.1, s32[1]{0:T(128)S(6)} %copy.6.refs_2_), custom_call_target="tpu_custom_call" | custom-call | tf_op jit(solution)/shard_map/link/pallas_call | solution.py:432
  28.3 1.0 %put.1 = f32[2400,128]{1,0:T(8,128)} custom-call(f32[2400,128]{1,0:T(8,128)S(1)} %link.1.in_ref), custom_call_target="tpu_custom_call" | custom-call | tf_op jit(solution)/shard_map/put/pallas_call | solution.py:473

commit v4 on v3

--- a/solution.py
+++ b/solution.py
@@ -10,6 +10,8 @@
 WIDTH = 2 * HALF + 1
 LANE = 128
 SUB = 16
+EIGHT = 8
+GROUP = 4
 VMEM_LIMIT = 32000000
 MESH = pl.DeviceIdType.MESH
 
@@ -20,14 +22,14 @@
 
 def kernel(
     n, ndate, x_hbm, mask_hbm, index_ref, out_ref,
-    raw, mask_ref, wide, scene, turned, chosen, picks, weight, pairs, coef, late, edges, total, vectors, gains, long_gain, column, powers, refs,
-    load_sem, mask_sem, far_sem, near_sem, power_sem, ref_sem,
+    raw, mask_ref, wide, scene, turned, chosen, picks, pieces, weight, pairs, coef, late, edges, total, vectors, gains, long_gain, column, powers, plane_rows, whole_row, refs,
+    load_sem, mask_sem, lane_sem, far_sem, near_sem, piece_sem, power_sem, plane_sem, whole_sem, ref_sem,
 ):
     _, rows, cols = mask_ref.shape
     span, blocks, depth, _ = scene.shape
     half = depth // 2
     tiles = turned.shape[1]
-    long_depth = refs.shape[3]
+    long_depth = refs.shape[2]
     long_dates = powers.shape[2]
     total_rows = rows * n
     stride = blocks * rows
@@ -45,11 +47,39 @@
     def place(q):
         return q + odd * (rows - 1 - 2 * q)
 
+    group = GROUP if n % GROUP == 0 else n
+    planes = n // group
+    plane = me // group
+    lane = lax.rem(me, group)
+    has_up = plane < planes - 1
+    has_down = plane > 0
+    crosses = has_far & ((lane + 1 - 2 * (1 - odd) < 0) | (lane + 1 - 2 * (1 - odd) > group - 1))
+
+    def signal(sem, target):
+        pl.semaphore_signal(sem, inc=1, device_id={"row": target}, device_id_type=MESH)
+
+    def signal_mates(sem):
+        for k in range(1, group):
+            signal(sem, plane * group + lax.rem(lane + k, group))
+
     barrier = pltpu.get_barrier_semaphore()
-
-    @pl.loop(1, n)
-    def _(k):
-        pl.semaphore_signal(barrier, inc=1, device_id={"row": peer(k)}, device_id_type=MESH)
+    pl.when(crosses)(lambda: signal(barrier, jnp.clip(far, 0, n - 1)))
+    pl.when(has_up)(lambda: signal(barrier, jnp.minimum(me + group, n - 1)))
+    pl.when(has_down)(lambda: signal(barrier, jnp.maximum(me - group, 0)))
+    signal_mates(barrier)
+    expected = group - 1 + has_up.astype(jnp.int32) + has_down.astype(jnp.int32) + crosses.astype(jnp.int32)
+
+    def meet_lane(d):
+        pl.when(has_up)(lambda: signal(lane_sem.at[0, d], jnp.minimum(me + group, n - 1)))
+        pl.when(has_down)(lambda: signal(lane_sem.at[1, d], jnp.maximum(me - group, 0)))
+
+        @pl.when(has_down)
+        def _():
+            pl.semaphore_wait(lane_sem.at[0, d], 1)
+
+        @pl.when(has_up)
+        def _():
+            pl.semaphore_wait(lane_sem.at[1, d], 1)
 
     load = pltpu.make_async_copy(x_hbm, raw, load_sem)
     load.start()
@@ -70,61 +100,135 @@
                 scene[HALF + q, block, part * half:(part + 1) * half, :] = piece.astype(jnp.bfloat16)
                 sums = sums + piece * piece
     column[0:half, :] = sums
-    powers[me] = jnp.sum(column[0:long_dates, :].T, axis=0, keepdims=True)
-
-    pl.semaphore_wait(barrier, n - 1)
-
-    def exchange(buffer, sems):
-        def copy(k, slot):
-            return pltpu.make_async_remote_copy(
-                src_ref=buffer.at[slot], dst_ref=buffer.at[slot],
-                send_sem=sems.at[0, k], recv_sem=sems.at[1, slot],
-                device_id={"row": peer(k)}, device_id_type=MESH,
-            )
-
-        def start():
-            for k in range(1, n):
-                copy(k, me).start()
-
-        def finish():
-            @pl.loop(1, n)
-            def _(k):
-                copy(k, peer(k)).wait_recv()
-
-            @pl.loop(1, n)
-            def _(k):
-                copy(k, me).wait_send()
-
-        return start, finish
-
-    start_power, finish_power = exchange(powers, power_sem)
-    start_power()
+    powers[lane] = jnp.sum(column[0:long_dates, :].T, axis=0, keepdims=True)
+
+    target = index_ref[0]
+    target_row = lax.div(target, cols) - first_row
+    target_col = lax.rem(target, cols)
+    base = jnp.clip(lax.div(target_col + SUB - HALF, SUB) - 1, 0, cols // SUB - 2)
+    home = lax.broadcasted_iota(jnp.int32, (1, long_depth), 1) * 0 + target_row
+
+    def turn(slot):
+        for block in range(blocks):
+            lines = slice(block * LANE, (block + 1) * LANE)
+            for i in range(tiles):
+                deep = slice(i * LANE, min((i + 1) * LANE, depth))
+                tile = scene[slot, block, deep, :]
+                if tile.shape[0] < LANE:
+                    tile = jnp.concatenate([tile, jnp.zeros((LANE - tile.shape[0], LANE), tile.dtype)], axis=0)
+                turned[slot, i, lines, :] = tile.T
+
+    def pick(slot):
+        group_of = lax.broadcasted_iota(jnp.int32, (SUB, LANE), 1) * 0 + base
+        hits = [(group_of == k).astype(jnp.float32).astype(scene.dtype) for k in range(-1, cols // SUB)]
+        strips = []
+        for i in range(tiles):
+            first = jnp.zeros((SUB, LANE), scene.dtype)
+            second = first
+            for k in range(cols // SUB):
+                piece = turned[slot, i, k * SUB:(k + 1) * SUB, :]
+                first = first + piece * hits[k + 1]
+                second = second + piece * hits[k]
+            strips.append(jnp.concatenate([first, second], axis=0))
+        shape = (SUB, 2 * SUB)
+        offset = lax.broadcasted_iota(jnp.int32, shape, 0)
+        line = lax.broadcasted_iota(jnp.int32, shape, 1)
+        hit = (line == target_col - HALF - base * SUB + offset) & (offset < WIDTH)
+        left = hit.astype(jnp.float32).astype(scene.dtype)
+        found = jnp.dot(left, jnp.concatenate(strips, axis=1), preferred_element_type=jnp.float32)
+        picks[slot] = found[0:EIGHT].astype(scene.dtype)
+
+    pl.semaphore_wait(barrier, expected)
+
+    def mate_copy(k, rows_sent):
+        return pltpu.make_async_remote_copy(
+            src_ref=powers.at[rows_sent], dst_ref=powers.at[rows_sent],
+            send_sem=power_sem.at[0], recv_sem=power_sem.at[1],
+            device_id={"row": plane * group + lax.rem(lane + k, group)}, device_id_type=MESH,
+        )
+
+    def plane_copy(k, rows_sent):
+        return pltpu.make_async_remote_copy(
+            src_ref=plane_rows.at[rows_sent], dst_ref=plane_rows.at[rows_sent],
+            send_sem=plane_sem.at[0], recv_sem=plane_sem.at[1],
+            device_id={"row": lax.rem(plane + k, planes) * group + lane}, device_id_type=MESH,
+        )
+
+    def ref_copy(k, rows_sent):
+        return pltpu.make_async_remote_copy(
+            src_ref=refs.at[rows_sent], dst_ref=refs.at[rows_sent],
+            send_sem=ref_sem.at[0], recv_sem=ref_sem.at[1],
+            device_id={"row": peer(k)}, device_id_type=MESH,
+        )
+
+    mate_all = mate_copy(1, pl.ds(0, group - 1))
+    ref_all = ref_copy(1, pl.ds(0, n - 1))
+    if planes > 1:
+        plane_all = plane_copy(1, pl.ds(0, planes - 1))
+
+    inner = (lane > 0) & (lane < group - 1) if planes > 1 else lane >= 0
+    outer = jnp.logical_not(inner)
 
     far_id = jnp.clip(far, 0, n - 1)
     near_id = jnp.clip(near, 0, n - 1)
 
-    def far_copy(t):
+    def far_copy(t, first, last):
+        chunk = pl.ds(first, last - first)
         return pltpu.make_async_remote_copy(
-            src_ref=scene.at[HALF + t], dst_ref=scene.at[HALF - 1 - t],
-            send_sem=far_sem.at[0, t], recv_sem=far_sem.at[1, t],
+            src_ref=scene.at[HALF + t, chunk], dst_ref=scene.at[HALF - 1 - t, chunk],
+            send_sem=far_sem.at[HALF], recv_sem=far_sem.at[t],
             device_id={"row": far_id}, device_id_type=MESH,
         )
 
     def near_copy(t):
         return pltpu.make_async_remote_copy(
             src_ref=scene.at[HALF + rows - 1 - t], dst_ref=scene.at[HALF + rows + t],
-            send_sem=near_sem.at[0, t], recv_sem=near_sem.at[1, t],
+            send_sem=near_sem.at[0], recv_sem=near_sem.at[1],
             device_id={"row": near_id}, device_id_type=MESH,
         )
 
-    for t in range(HALF):
-        pl.when(has_far)(far_copy(t).start)
+    near_all = pltpu.make_async_remote_copy(
+        src_ref=scene.at[pl.ds(HALF + rows - HALF, HALF)], dst_ref=scene.at[pl.ds(HALF + rows, HALF)],
+        send_sem=near_sem.at[0], recv_sem=near_sem.at[1],
+        device_id={"row": near_id}, device_id_type=MESH,
+    )
+    far_all = pltpu.make_async_remote_copy(
+        src_ref=scene.at[pl.ds(HALF, HALF)], dst_ref=scene.at[pl.ds(0, HALF)],
+        send_sem=far_sem.at[HALF], recv_sem=far_sem.at[0],
+        device_id={"row": far_id}, device_id_type=MESH,
+    )
+    piece_copy = pltpu.make_async_remote_copy(
+        src_ref=pieces, dst_ref=picks.at[pl.ds(0, HALF)],
+        send_sem=piece_sem.at[0], recv_sem=piece_sem.at[1],
+        device_id={"row": far_id}, device_id_type=MESH,
+    )
+
+    def send_rest():
+        piece_copy.start()
+        far_copy(0, 1, blocks).start()
+        for t in range(1, HALF):
+            far_copy(t, 0, blocks).start()
+
+    whole_copy = pltpu.make_async_remote_copy(
+        src_ref=whole_row, dst_ref=whole_row, send_sem=whole_sem.at[0], recv_sem=whole_sem.at[1],
+        device_id={"row": near_id}, device_id_type=MESH,
+    )
+    for k in range(1, group):
+        mate_copy(k, lane).start()
+    pl.when(inner & has_far)(far_copy(0, 0, 1).start)
     for t in range(HALF):
         pl.when(has_near)(near_copy(t).start)
+    for q in range(rows):
+        turn(HALF + q)
+        pick(HALF + q)
+    for t in range(HALF):
+        pieces[HALF - 1 - t] = picks[HALF + t]
+    pl.when(inner & has_far)(send_rest)
 
     @pl.when(jnp.logical_not(has_far))
     def _():
         scene[0:HALF] = jnp.zeros((HALF, blocks, depth, LANE), scene.dtype)
+        picks[0:HALF] = jnp.zeros((HALF, EIGHT, long_depth), scene.dtype)
 
     @pl.when(jnp.logical_not(has_near))
     def _():
@@ -147,12 +251,12 @@
             ones.append(one)
             count = count + one
     inverse = 1.0 / (count * ndate)
+    chosen[...] = jnp.zeros_like(chosen)
     for o in range(WIDTH * WIDTH):
         line = ones[o] * inverse
         for q in range(rows):
-            chosen[q, o:o + 1, :] = jnp.where(odd == 1, line[rows - 1 - q:rows - q], line[q:q + 1])
-    for q in range(rows):
-        chosen[q, WIDTH * WIDTH:, :] = jnp.zeros((chosen.shape[1] - WIDTH * WIDTH, cols), jnp.float32)
+            spot = o // WIDTH * EIGHT + o % WIDTH
+            chosen[q, spot:spot + 1, :] = jnp.where(odd == 1, line[rows - 1 - q:rows - q], line[q:q + 1])
 
     def window(block):
         return max(0, block * LANE - SUB), min(cols, (block + 1) * LANE + SUB)
@@ -168,36 +272,9 @@
             for a in range(WIDTH):
                 band = jnp.zeros(shape, jnp.float32)
                 for b in range(WIDTH):
-                    line = chosen[q, a * WIDTH + b:a * WIDTH + b + 1, block * LANE:(block + 1) * LANE]
+                    line = chosen[q, a * EIGHT + b:a * EIGHT + b + 1, block * LANE:(block + 1) * LANE]
                     band = jnp.where(shift == b - HALF, line, band)
                 weight[block, q, a, 0:end - begin, :] = band
-
-    target = index_ref[0]
-    target_row = lax.div(target, cols) - first_row
-    target_col = lax.rem(target, cols)
-    base = jnp.clip(lax.div(target_col + SUB - HALF, SUB) - 1, 0, cols // SUB - 2)
-    home = lax.broadcasted_iota(jnp.int32, (1, long_depth), 1) * 0 + target_row
-
-    def turn(slot):
-        for block in range(blocks):
-            lines = slice(block * LANE, (block + 1) * LANE)
-            for i in range(tiles):
-                deep = slice(i * LANE, min((i + 1) * LANE, depth))
-                tile = scene[slot, block, deep, :]
-                if tile.shape[0] < LANE:
-                    tile = jnp.concatenate([tile, jnp.zeros((LANE - tile.shape[0], LANE), tile.dtype)], axis=0)
-                turned[slot, i, lines, :] = tile.T
-        group = lax.broadcasted_iota(jnp.int32, (SUB, LANE), 1) * 0 + base
-        hits = [(group == k).astype(jnp.float32).astype(scene.dtype) for k in range(-1, cols // SUB)]
-        for i in range(tiles):
-            first = jnp.zeros((SUB, LANE), scene.dtype)
-            second = first
-            for k in range(cols // SUB):
-                piece = turned[slot, i, k * SUB:(k + 1) * SUB, :]
-                first = first + piece * hits[k + 1]
-                second = second + piece * hits[k]
-            picks[slot, i, 0:SUB, :] = first
-            picks[slot, i, SUB:2 * SUB, :] = second
 
     def sides(block):
         ends = []
@@ -221,11 +298,30 @@
                     parts.append(jnp.zeros((edges.shape[2] - used, LANE), edges.dtype))
                 edges[block, i * LANE:(i + 1) * LANE, :] = jnp.concatenate(parts, axis=0).T
 
-    for q in range(rows):
-        turn(HALF + q)
-
-    finish_power()
-    power = jnp.sum(powers[...], axis=0)
+    mate_all.wait_recv()
+    if planes > 1:
+        @pl.when(outer & has_far)
+        def _():
+            far_copy(0, 0, 1).start()
+            send_rest()
+    plane_rows[plane] = jnp.sum(powers[...], axis=0)
+    if planes > 1:
+        @pl.when(inner)
+        def _():
+            for d in range(planes - 2):
+                meet_lane(d)
+            for k in range(1, planes):
+                plane_copy(k, plane).start()
+            plane_all.wait_recv()
+            whole_row[...] = jnp.sum(plane_rows[...], axis=0)
+            whole_copy.start()
+
+        @pl.when(outer)
+        def _():
+            whole_copy.wait_recv()
+    else:
+        whole_row[...] = plane_rows[0]
+    power = whole_row[...]
     gain_row = lax.rsqrt(power * (1.0 / (total_rows * cols)) + 0.1)
     gains[...] = jnp.broadcast_to(gain_row, (LANE, long_dates)).T[0:half, :]
     tall = jnp.concatenate([gains[...], gains[...], jnp.zeros((long_depth - depth, LANE), jnp.float32)], axis=0)
@@ -310,9 +406,11 @@
     def seen(q, slots):
         return [s for s in slots if q <= s < q + WIDTH]
 
+    pl.when(has_near)(near_all.wait_recv)
+    pl.when(has_far)(piece_copy.wait_recv)
     for t in range(HALF):
-        pl.when(has_near)(near_copy(t).wait_recv)
         turn(HALF + rows + t)
+        pick(HALF + rows + t)
     set_edges(HALF)
     for q in range(rows):
         slots = seen(q, range(HALF, span))
@@ -328,19 +426,10 @@
         return jnp.where(lanes < half, -ahead, jnp.where(lanes < depth, behind, 0.0))
 
     def reference_vector(q):
-        shape = (2 * SUB, WIDTH * 2 * SUB)
-        offset = lax.broadcasted_iota(jnp.int32, shape, 0)
-        line = lax.broadcasted_iota(jnp.int32, shape, 1)
-        hit = line - (offset // WIDTH) * (2 * SUB) == target_col - HALF - base * SUB + offset % WIDTH
-        hit = hit & (line // (2 * SUB) == offset // WIDTH)
-        left = hit.astype(jnp.float32).astype(jnp.bfloat16)
-        right = jnp.concatenate(
-            [jnp.concatenate([picks[q + a, i] for i in range(tiles)], axis=1) for a in range(WIDTH)], axis=0
-        )
-        stack = jnp.dot(left, right, preferred_element_type=jnp.float32)
-        lanes = lax.broadcasted_iota(jnp.int32, (2 * SUB, cols), 1)
+        stack = jnp.concatenate([picks[q + a].astype(jnp.float32) for a in range(WIDTH)], axis=0)
+        lanes = lax.broadcasted_iota(jnp.int32, (WIDTH * EIGHT, cols), 1)
         bands = jnp.sum(jnp.where(lanes == target_col, chosen[q], 0.0), axis=1, keepdims=True)
-        middle = HALF * WIDTH + HALF
+        middle = HALF * EIGHT + HALF
         center = stack[middle:middle + 1]
         gain = long_gain[0:1, :]
         vector = center * gain
@@ -355,29 +444,22 @@
             vector = vector * lax.rsqrt(energy * (1.0 / ndate) + 0.001)
         return vector
 
-    finish = []
-
-    def set_reference(q):
-        refs[q, me] = jnp.where(home == place(q), reference_vector(q), 0.0)
-
-    def send_reference(q):
-        start, end = exchange(refs.at[q], ref_sem.at[q])
-        start()
-        finish.append(end)
+    found = jnp.zeros((1, long_depth), jnp.float32)
+    for q in range(rows):
+        found = found + jnp.where(home == place(q), reference_vector(q), 0.0)
+    refs[me] = found
+    for k in range(1, n):
+        ref_copy(k, me).start()
 
     for q in range(HALF, rows):
-        set_reference(q)
-        send_reference(q)
         for block in range(blocks):
             first_step(q, block, total[q, block])
         last_steps(q)
     for t in range(HALF):
         slot = HALF - 1 - t
-        pl.when(has_far)(far_copy(t).wait_recv)
+        pl.when(has_far)(far_copy(t, 0, blocks).wait_recv)
         turn(slot)
         set_edges(slot)
-        if slot < rows:
-            set_reference(slot)
         for q in range(min(slot, rows - 1), -1, -1):
             for block in range(blocks):
                 project(q, block, [slot], into_late=True)
@@ -385,15 +467,13 @@
             products = [late_update(slot, block, slot) for block in range(blocks)]
             for block in range(blocks):
                 first_step(slot, block, total[slot, block] + products[block])
-            send_reference(slot)
             last_steps(slot)
         for q in range(min(slot, rows) - 1, -1, -1):
             for block in range(blocks):
                 total[q, block] += late_update(q, block, slot)
 
-    for end in finish:
-        end()
-    refvec = jnp.sum(jnp.sum(refs[...], axis=0), axis=0)
+    ref_all.wait_recv()
+    refvec = jnp.sum(refs[...], axis=0)
     refvec = jnp.broadcast_to(refvec, (LANE, long_depth)).T
     ref_real = refvec[0:half]
     ref_imag = refvec[half:depth]
@@ -406,14 +486,22 @@
             start = start + ndate * stride
             out_ref[pl.ds(start, ndate, stride=stride), :] = (imag * ref_real - real * ref_imag)[0:ndate]
 
-    for t in range(HALF):
-        pl.when(has_far)(far_copy(t).wait_send)
-        pl.when(has_near)(near_copy(t).wait_send)
+    pl.when(has_far)(far_all.wait_send)
+    pl.when(has_far)(piece_copy.wait_send)
+    pl.when(has_near)(near_all.wait_send)
+    mate_all.wait_send()
+    ref_all.wait_send()
+    if planes > 1:
+        @pl.when(inner)
+        def _():
+            plane_all.wait_send()
+            whole_copy.wait_send()
 
 
 def per_device(slc, mask, ref_index):
     parts, ndate, rows, cols = slc.shape
     n = lax.axis_size("row")
+    group = GROUP if n % GROUP == 0 else n
     half = round_up(ndate, SUB)
     depth = 2 * half
     long_dates = round_up(half, LANE)
@@ -440,8 +528,9 @@
             pltpu.VMEM((lines + (half - ndate) * blocks * rows, LANE), jnp.float32),
             pltpu.VMEM((span, blocks, depth, LANE), jnp.bfloat16),
             pltpu.VMEM((span, long_depth // LANE, cols, LANE), jnp.bfloat16),
-            pltpu.VMEM((rows, 2 * SUB, cols), jnp.float32),
-            pltpu.VMEM((span, long_depth // LANE, 2 * SUB, LANE), jnp.bfloat16),
+            pltpu.VMEM((rows, WIDTH * EIGHT, cols), jnp.float32),
+            pltpu.VMEM((span, EIGHT, long_depth), jnp.bfloat16),
+            pltpu.VMEM((HALF, EIGHT, long_depth), jnp.bfloat16),
             pltpu.VMEM((blocks, rows, WIDTH, LANE + 2 * SUB, LANE), jnp.float32),
             pltpu.VMEM((rows, blocks, 2, depth, LANE), jnp.bfloat16),
             pltpu.VMEM((rows, blocks, 2, WIDTH * LANE + margin, LANE), jnp.bfloat16),
@@ -452,14 +541,20 @@
             pltpu.VMEM((half, LANE), jnp.float32),
             pltpu.VMEM((8, long_depth), jnp.float32),
             pltpu.VMEM((long_depth, LANE), jnp.float32),
-            pltpu.VMEM((n, 1, long_dates), jnp.float32),
-            pltpu.VMEM((rows, n, 1, long_depth), jnp.float32),
+            pltpu.VMEM((group, 1, long_dates), jnp.float32),
+            pltpu.VMEM((n // group, 1, long_dates), jnp.float32),
+            pltpu.VMEM((1, long_dates), jnp.float32),
+            pltpu.VMEM((n, 1, long_depth), jnp.float32),
             pltpu.SemaphoreType.DMA,
             pltpu.SemaphoreType.DMA,
-            pltpu.SemaphoreType.DMA((2, HALF)),
-            pltpu.SemaphoreType.DMA((2, HALF)),
-            pltpu.SemaphoreType.DMA((2, n)),
-            pltpu.SemaphoreType.DMA((rows, 2, n)),
+            pltpu.SemaphoreType.REGULAR((2, max(1, n // group - 2))),
+            pltpu.SemaphoreType.DMA((HALF + 1,)),
+            pltpu.SemaphoreType.DMA((2,)),
+            pltpu.SemaphoreType.DMA((2,)),
+            pltpu.SemaphoreType.DMA((2,)),
+            pltpu.SemaphoreType.DMA((2,)),
+            pltpu.SemaphoreType.DMA((2,)),
+            pltpu.SemaphoreType.DMA((2,)),
         ],
         compiler_params=pltpu.CompilerParams(collective_id=0, has_side_effects=True, vmem_limit_bytes=VMEM_LIMIT),
         name="link",

time: 29.5 us -> 23.9 us (0.81)
  Pallas kernels: 28.7 us -> 23.1 us
    pallas_call x1, Pallas kernels: 27.7 us -> 22.1 us  [per_device(): pl.pallas_call(body, out_shape=jax.ShapeDtypeStruct((lines, LANE), jnp.fl...]
where the time goes in v4:
time: 23.9 us; the launch traced here: 23.8 us
  Pallas kernels  23.1 us (97%)
  between operations  0.66 us (3%)
    pallas_call x1, Pallas kernels, per_device(): pl.pallas_call(body, out_shape=jax.ShapeDtypeStruct((lines, LANE), jnp.fl...  22.1 us
    pallas_call x1, Pallas kernels, per_device(): pl.pallas_call(put, out_shape=jax.ShapeDtypeStruct((lines, LANE), jnp.flo...  1.04 us

profile of v4, /device:TPU:0, one launch (start us, length us, event | category | flops | bytes accessed | tf_op | source)
XLA Modules:
  0.0 23.8 jit_solution(1145184439646823780)
XLA Ops:
  0.7 22.1 %link.1.in_ref = f32[2400,128]{1,0:T(8,128)S(1)} custom-call(bf16[2400,128]{1,0:T(8,128)(2,1)} %bitcast.10, s32[25,2,256]{2,1,0:T(2,128)} %refs_1_.1, s32[1]{0:T(128)S(6)} %copy.6.refs_2_), custom_call_target="tpu_custom_call" | custom-call | tf_op jit(solution)/shard_map/link/pallas_call | solution.py:520
  22.8 1.0 %put.1 = f32[2400,128]{1,0:T(8,128)} custom-call(f32[2400,128]{1,0:T(8,128)S(1)} %link.1.in_ref), custom_call_target="tpu_custom_call" | custom-call | tf_op jit(solution)/shard_map/put/pallas_call | solution.py:568

commit v5 on v4

--- a/solution.py
+++ b/solution.py
@@ -12,6 +12,7 @@
 SUB = 16
 EIGHT = 8
 GROUP = 4
+PUTS = 4
 VMEM_LIMIT = 32000000
 MESH = pl.DeviceIdType.MESH
 
@@ -47,6 +48,16 @@
     def place(q):
         return q + odd * (rows - 1 - 2 * q)
 
+    part_rows = raw.shape[0] // 2
+
+    def load(part):
+        chunk = pl.ds(part * part_rows, part_rows)
+        return pltpu.make_async_copy(x_hbm.at[chunk], raw.at[chunk], load_sem.at[part])
+
+    for part in range(2):
+        load(part).start()
+    load_mask = pltpu.make_async_copy(mask_hbm, mask_ref, mask_sem)
+    load_mask.start()
     group = GROUP if n % GROUP == 0 else n
     planes = n // group
     plane = me // group
@@ -81,20 +92,17 @@
         def _():
             pl.semaphore_wait(lane_sem.at[1, d], 1)
 
-    load = pltpu.make_async_copy(x_hbm, raw, load_sem)
-    load.start()
-    load_mask = pltpu.make_async_copy(mask_hbm, mask_ref, mask_sem)
-    load_mask.start()
     column[...] = jnp.zeros_like(column)
 
-    load.wait()
-    wide[0:raw.shape[0], :] = raw[...].astype(jnp.float32)
     sums = jnp.zeros((half, LANE), jnp.float32)
     dates = lax.broadcasted_iota(jnp.int32, (half, LANE), 0)
-    for q in range(rows):
-        for part in range(2):
+    for part in range(2):
+        load(part).wait()
+        chunk = slice(part * part_rows, (part + 1) * part_rows)
+        wide[chunk, :] = raw[chunk, :].astype(jnp.float32)
+        for q in range(rows):
             for block in range(blocks):
-                start = part * ndate * stride + block * rows + place(q)
+                start = part * part_rows + block * rows + place(q)
                 piece = wide[pl.ds(start, half, stride=stride), :]
                 piece = jnp.where(dates < ndate, piece, 0.0)
                 scene[HALF + q, block, part * half:(part + 1) * half, :] = piece.astype(jnp.bfloat16)
@@ -172,13 +180,14 @@
     far_id = jnp.clip(far, 0, n - 1)
     near_id = jnp.clip(near, 0, n - 1)
 
-    def far_copy(t, first, last):
-        chunk = pl.ds(first, last - first)
+    def far_copy(t, chunk=slice(None), deep=slice(None)):
         return pltpu.make_async_remote_copy(
-            src_ref=scene.at[HALF + t, chunk], dst_ref=scene.at[HALF - 1 - t, chunk],
+            src_ref=scene.at[HALF + t, chunk, deep], dst_ref=scene.at[HALF - 1 - t, chunk, deep],
             send_sem=far_sem.at[HALF], recv_sem=far_sem.at[t],
             device_id={"row": far_id}, device_id_type=MESH,
         )
+
+    far_first = far_copy(0, pl.ds(0, 1), pl.ds(0, half))
 
     def near_copy(t):
         return pltpu.make_async_remote_copy(
@@ -205,9 +214,10 @@
 
     def send_rest():
         piece_copy.start()
-        far_copy(0, 1, blocks).start()
+        far_copy(0, pl.ds(0, 1), pl.ds(half, half)).start()
+        far_copy(0, pl.ds(1, blocks - 1)).start()
         for t in range(1, HALF):
-            far_copy(t, 0, blocks).start()
+            far_copy(t).start()
 
     whole_copy = pltpu.make_async_remote_copy(
         src_ref=whole_row, dst_ref=whole_row, send_sem=whole_sem.at[0], recv_sem=whole_sem.at[1],
@@ -215,7 +225,7 @@
     )
     for k in range(1, group):
         mate_copy(k, lane).start()
-    pl.when(inner & has_far)(far_copy(0, 0, 1).start)
+    pl.when(inner & has_far)(far_first.start)
     for t in range(HALF):
         pl.when(has_near)(near_copy(t).start)
     for q in range(rows):
@@ -302,7 +312,7 @@
     if planes > 1:
         @pl.when(outer & has_far)
         def _():
-            far_copy(0, 0, 1).start()
+            far_first.start()
             send_rest()
     plane_rows[plane] = jnp.sum(powers[...], axis=0)
     if planes > 1:
@@ -341,7 +351,7 @@
                 q, block, (tile[0:half] * square).astype(jnp.bfloat16), (tile[half:depth] * square).astype(jnp.bfloat16)
             )
 
-    def project(q, block, slots, into_late=False):
+    def project(q, block, slots, into_late=False, factor=None):
         begin, end = window(block)
         size = end - begin
         main = block * LANE - begin
@@ -353,6 +363,8 @@
         for i, slot in enumerate(slots):
             a = slot - q
             band = weight[block, q, a, 0:size, :]
+            if factor is not None:
+                band = band * factor
             for c in range(2):
                 part = (proj[i * size:(i + 1) * size, c * LANE:(c + 1) * LANE] * band).astype(jnp.bfloat16)
                 if into_late:
@@ -374,34 +386,32 @@
         right = jnp.concatenate([late[q, block, 0], late[q, block, 1]], axis=1)
         return jnp.dot(left, right, preferred_element_type=jnp.float32)
 
-    def normalize(product):
+    def combine(product):
         gain = gains[...]
         top, bottom = product[0:half], product[half:depth]
         real = (top[:, 0:LANE] - bottom[:, LANE:2 * LANE]) * gain
         imag = (top[:, LANE:2 * LANE] + bottom[:, 0:LANE]) * gain
         energy = jnp.sum(real * real + imag * imag, axis=0, keepdims=True)
-        factor = lax.rsqrt(energy * (1.0 / ndate) + 0.001)
-        return real * factor, imag * factor
+        return real, imag, lax.rsqrt(energy * (1.0 / ndate) + 0.001)
 
     def first_step(q, block, product):
-        real, imag = normalize(product)
+        real, imag, factor = combine(product)
         gain = gains[...]
         set_pair(q, block, (real * gain).astype(jnp.bfloat16), (imag * gain).astype(jnp.bfloat16))
-
-    def last_steps(q):
+        return factor
+
+    def last_steps(q, factors):
         window_slots = list(range(q, q + WIDTH))
         for i in range(1, ITERS):
             for block in range(blocks):
-                project(q, block, window_slots)
+                project(q, block, window_slots, factor=factors[block])
             products = [update(q, block, window_slots) for block in range(blocks)]
-            for block in range(blocks):
-                real, imag = normalize(products[block])
-                if i < ITERS - 1:
-                    gain = gains[...]
-                    set_pair(q, block, (real * gain).astype(jnp.bfloat16), (imag * gain).astype(jnp.bfloat16))
-                else:
-                    vectors[q, block, 0:half, :] = real
-                    vectors[q, block, half:depth, :] = imag
+            if i < ITERS - 1:
+                factors = [first_step(q, block, products[block]) for block in range(blocks)]
+        for block in range(blocks):
+            real, imag, factor = combine(products[block])
+            vectors[q, block, 0:half, :] = real * factor
+            vectors[q, block, half:depth, :] = imag * factor
 
     def seen(q, slots):
         return [s for s in slots if q <= s < q + WIDTH]
@@ -452,12 +462,10 @@
         ref_copy(k, me).start()
 
     for q in range(HALF, rows):
-        for block in range(blocks):
-            first_step(q, block, total[q, block])
-        last_steps(q)
+        last_steps(q, [first_step(q, block, total[q, block]) for block in range(blocks)])
     for t in range(HALF):
         slot = HALF - 1 - t
-        pl.when(has_far)(far_copy(t, 0, blocks).wait_recv)
+        pl.when(has_far)(far_copy(t).wait_recv)
         turn(slot)
         set_edges(slot)
         for q in range(min(slot, rows - 1), -1, -1):
@@ -465,9 +473,8 @@
                 project(q, block, [slot], into_late=True)
         if slot < rows:
             products = [late_update(slot, block, slot) for block in range(blocks)]
-            for block in range(blocks):
-                first_step(slot, block, total[slot, block] + products[block])
-            last_steps(slot)
+            factors = [first_step(slot, block, total[slot, block] + products[block]) for block in range(blocks)]
+            last_steps(slot, factors)
         for q in range(min(slot, rows) - 1, -1, -1):
             for block in range(blocks):
                 total[q, block] += late_update(q, block, slot)
@@ -545,7 +552,7 @@
             pltpu.VMEM((n // group, 1, long_dates), jnp.float32),
             pltpu.VMEM((1, long_dates), jnp.float32),
             pltpu.VMEM((n, 1, long_depth), jnp.float32),
-            pltpu.SemaphoreType.DMA,
+            pltpu.SemaphoreType.DMA((2,)),
             pltpu.SemaphoreType.DMA,
             pltpu.SemaphoreType.REGULAR((2, max(1, n // group - 2))),
             pltpu.SemaphoreType.DMA((HALF + 1,)),
@@ -561,16 +568,23 @@
     )(pltpu.with_memory_space_constraint(x, pltpu.HBM), pltpu.with_memory_space_constraint(mask, pltpu.HBM), ref_index)
 
     def put(in_ref, out_ref, sem):
-        copy = pltpu.make_async_copy(in_ref, out_ref, sem)
-        copy.start()
-        copy.wait()
+        size = lines // PUTS // EIGHT * EIGHT
+        ends = [k * size for k in range(PUTS)] + [lines]
+        copies = []
+        for k in range(PUTS):
+            chunk = pl.ds(ends[k], ends[k + 1] - ends[k])
+            copies.append(pltpu.make_async_copy(in_ref.at[chunk], out_ref.at[chunk], sem.at[k]))
+        for copy in copies:
+            copy.start()
+        for copy in copies:
+            copy.wait()
 
     out = pl.pallas_call(
         put,
         out_shape=jax.ShapeDtypeStruct((lines, LANE), jnp.float32),
         in_specs=[vmem],
         out_specs=anywhere,
-        scratch_shapes=[pltpu.SemaphoreType.DMA],
+        scratch_shapes=[pltpu.SemaphoreType.DMA((PUTS,))],
         compiler_params=pltpu.CompilerParams(vmem_limit_bytes=16 * 1024 * 1024),
         name="put",
     )(out)

time: 23.9 us -> 23.3 us (0.975)
  the two profiles are of different devices: /device:TPU:0 before, /device:TPU:9 now
where the time goes in v5:
time: 23.3 us; the launch traced here: 23.2 us
  Pallas kernels  22.5 us (97%)
  between operations  0.66 us (3%)
    pallas_call x1, Pallas kernels, per_device(): pl.pallas_call(body, out_shape=jax.ShapeDtypeStruct((lines, LANE), jnp.fl...  21.5 us
    pallas_call x1, Pallas kernels, per_device(): pl.pallas_call(put, out_shape=jax.ShapeDtypeStruct((lines, LANE), jnp.flo...  1.06 us

profile of v5, /device:TPU:9, one launch (start us, length us, event | category | flops | bytes accessed | tf_op | source)
XLA Modules:
  0.0 23.2 jit_solution(10755305516251762146)
XLA Ops:
  0.7 21.5 %link.1.in_ref = f32[2400,128]{1,0:T(8,128)S(1)} custom-call(bf16[2400,128]{1,0:T(8,128)(2,1)} %bitcast.10, s32[25,2,256]{2,1,0:T(2,128)} %refs_1_.1, s32[1]{0:T(128)S(6)} %copy.6.refs_2_), custom_call_target="tpu_custom_call" | custom-call | tf_op jit(solution)/shard_map/link/pallas_call | solution.py:527
  22.1 1.1 %put.1 = f32[2400,128]{1,0:T(8,128)} custom-call(f32[2400,128]{1,0:T(8,128)S(1)} %link.1.in_ref), custom_call_target="tpu_custom_call" | custom-call | tf_op jit(solution)/shard_map/put/pallas_call | solution.py:582

commit v6 on v5

--- a/solution.py
+++ b/solution.py
@@ -12,7 +12,7 @@
 SUB = 16
 EIGHT = 8
 GROUP = 4
-PUTS = 4
+PUTS = 3
 VMEM_LIMIT = 32000000
 MESH = pl.DeviceIdType.MESH
 
@@ -22,9 +22,9 @@
 
 
 def kernel(
-    n, ndate, x_hbm, mask_hbm, index_ref, out_ref,
-    raw, mask_ref, wide, scene, turned, chosen, picks, pieces, weight, pairs, coef, late, edges, total, vectors, gains, long_gain, column, powers, plane_rows, whole_row, refs,
-    load_sem, mask_sem, lane_sem, far_sem, near_sem, piece_sem, power_sem, plane_sem, whole_sem, ref_sem,
+    n, ndate, x_hbm, mask_hbm, index_hbm, vectors, columns,
+    raw, mask_ref, index_ref, wide, scene, turned, chosen, picks, pieces, weight, pairs, coef, late, edges, total, gains, long_gain, column, powers, plane_rows, whole_row, refs,
+    load_sem, mask_sem, index_sem, lane_sem, far_sem, near_sem, piece_sem, power_sem, plane_sem, whole_sem, ref_sem,
 ):
     _, rows, cols = mask_ref.shape
     span, blocks, depth, _ = scene.shape
@@ -58,6 +58,8 @@
         load(part).start()
     load_mask = pltpu.make_async_copy(mask_hbm, mask_ref, mask_sem)
     load_mask.start()
+    load_index = pltpu.make_async_copy(index_hbm, index_ref, index_sem)
+    load_index.start()
     group = GROUP if n % GROUP == 0 else n
     planes = n // group
     plane = me // group
@@ -110,6 +112,7 @@
     column[0:half, :] = sums
     powers[lane] = jnp.sum(column[0:long_dates, :].T, axis=0, keepdims=True)
 
+    load_index.wait()
     target = index_ref[0]
     target_row = lax.div(target, cols) - first_row
     target_col = lax.rem(target, cols)
@@ -226,8 +229,6 @@
     for k in range(1, group):
         mate_copy(k, lane).start()
     pl.when(inner & has_far)(far_first.start)
-    for t in range(HALF):
-        pl.when(has_near)(near_copy(t).start)
     for q in range(rows):
         turn(HALF + q)
         pick(HALF + q)
@@ -308,6 +309,8 @@
                     parts.append(jnp.zeros((edges.shape[2] - used, LANE), edges.dtype))
                 edges[block, i * LANE:(i + 1) * LANE, :] = jnp.concatenate(parts, axis=0).T
 
+    for t in range(HALF):
+        pl.when(has_near)(near_copy(t).start)
     mate_all.wait_recv()
     if planes > 1:
         @pl.when(outer & has_far)
@@ -410,8 +413,8 @@
                 factors = [first_step(q, block, products[block]) for block in range(blocks)]
         for block in range(blocks):
             real, imag, factor = combine(products[block])
-            vectors[q, block, 0:half, :] = real * factor
-            vectors[q, block, half:depth, :] = imag * factor
+            vectors[place(q), block, 0:half, :] = real * factor
+            vectors[place(q), block, half:depth, :] = imag * factor
 
     def seen(q, slots):
         return [s for s in slots if q <= s < q + WIDTH]
@@ -481,17 +484,7 @@
 
     ref_all.wait_recv()
     refvec = jnp.sum(refs[...], axis=0)
-    refvec = jnp.broadcast_to(refvec, (LANE, long_depth)).T
-    ref_real = refvec[0:half]
-    ref_imag = refvec[half:depth]
-    for q in range(rows):
-        for block in range(blocks):
-            real = vectors[q, block, 0:half, :]
-            imag = vectors[q, block, half:depth, :]
-            start = block * rows + place(q)
-            out_ref[pl.ds(start, ndate, stride=stride), :] = (real * ref_real + imag * ref_imag)[0:ndate]
-            start = start + ndate * stride
-            out_ref[pl.ds(start, ndate, stride=stride), :] = (imag * ref_real - real * ref_imag)[0:ndate]
+    columns[...] = jnp.broadcast_to(refvec, (LANE, long_depth)).T[0:depth]
 
     pl.when(has_far)(far_all.wait_send)
     pl.when(has_far)(piece_copy.wait_send)
@@ -524,14 +517,21 @@
     def body(*refs):
         kernel(n, ndate, *refs)
 
-    out = pl.pallas_call(
+    def in_hbm(array):
+        return pltpu.with_memory_space_constraint(array, pltpu.HBM)
+
+    vectors, columns = pl.pallas_call(
         body,
-        out_shape=jax.ShapeDtypeStruct((lines, LANE), jnp.float32),
-        in_specs=[anywhere, anywhere, pl.BlockSpec(memory_space=pltpu.SMEM)],
-        out_specs=vmem,
+        out_shape=(
+            jax.ShapeDtypeStruct((rows, blocks, depth, LANE), jnp.float32),
+            jax.ShapeDtypeStruct((depth, LANE), jnp.float32),
+        ),
+        in_specs=[anywhere, anywhere, anywhere],
+        out_specs=(vmem, vmem),
         scratch_shapes=[
             pltpu.VMEM((lines, LANE), jnp.bfloat16),
             pltpu.VMEM(mask.shape, jnp.int32),
+            pltpu.SMEM(ref_index.shape, jnp.int32),
             pltpu.VMEM((lines + (half - ndate) * blocks * rows, LANE), jnp.float32),
             pltpu.VMEM((span, blocks, depth, LANE), jnp.bfloat16),
             pltpu.VMEM((span, long_depth // LANE, cols, LANE), jnp.bfloat16),
@@ -544,7 +544,6 @@
             pltpu.VMEM((rows, blocks, 2, cols, LANE), jnp.bfloat16),
             pltpu.VMEM((blocks, long_depth, margin), jnp.bfloat16),
             pltpu.VMEM((rows, blocks, depth, 2 * LANE), jnp.float32),
-            pltpu.VMEM((rows, blocks, depth, LANE), jnp.float32),
             pltpu.VMEM((half, LANE), jnp.float32),
             pltpu.VMEM((8, long_depth), jnp.float32),
             pltpu.VMEM((long_depth, LANE), jnp.float32),
@@ -553,6 +552,7 @@
             pltpu.VMEM((1, long_dates), jnp.float32),
             pltpu.VMEM((n, 1, long_depth), jnp.float32),
             pltpu.SemaphoreType.DMA((2,)),
+            pltpu.SemaphoreType.DMA,
             pltpu.SemaphoreType.DMA,
             pltpu.SemaphoreType.REGULAR((2, max(1, n // group - 2))),
             pltpu.SemaphoreType.DMA((HALF + 1,)),
@@ -565,29 +565,40 @@
         ],
         compiler_params=pltpu.CompilerParams(collective_id=0, has_side_effects=True, vmem_limit_bytes=VMEM_LIMIT),
         name="link",
-    )(pltpu.with_memory_space_constraint(x, pltpu.HBM), pltpu.with_memory_space_constraint(mask, pltpu.HBM), ref_index)
-
-    def put(in_ref, out_ref, sem):
-        size = lines // PUTS // EIGHT * EIGHT
-        ends = [k * size for k in range(PUTS)] + [lines]
+    )(in_hbm(x), in_hbm(mask), ref_index)
+
+    def put(vectors, columns, out_ref, stage, sem):
+        size = round_up(ndate // PUTS, EIGHT)
         copies = []
         for k in range(PUTS):
-            chunk = pl.ds(ends[k], ends[k + 1] - ends[k])
-            copies.append(pltpu.make_async_copy(in_ref.at[chunk], out_ref.at[chunk], sem.at[k]))
-        for copy in copies:
-            copy.start()
+            first, last = k * size, min((k + 1) * size, ndate)
+            low, high = slice(first, last), slice(half + first, half + last)
+            ref_real, ref_imag = columns[low, :], columns[high, :]
+            for block in range(blocks):
+                for row in range(rows):
+                    real, imag = vectors[row, block, low, :], vectors[row, block, high, :]
+                    start = (first * blocks + block) * rows + row
+                    stride = blocks * rows
+                    stage[pl.ds(start, last - first, stride=stride), :] = real * ref_real + imag * ref_imag
+                    start = start + ndate * stride
+                    stage[pl.ds(start, last - first, stride=stride), :] = imag * ref_real - real * ref_imag
+            for part in range(parts):
+                chunk = pl.ds((part * ndate + first) * blocks * rows, (last - first) * blocks * rows)
+                copy = pltpu.make_async_copy(stage.at[chunk], out_ref.at[chunk], sem.at[k, part])
+                copy.start()
+                copies.append(copy)
         for copy in copies:
             copy.wait()
 
     out = pl.pallas_call(
         put,
         out_shape=jax.ShapeDtypeStruct((lines, LANE), jnp.float32),
-        in_specs=[vmem],
+        in_specs=[vmem, vmem],
         out_specs=anywhere,
-        scratch_shapes=[pltpu.SemaphoreType.DMA((PUTS,))],
+        scratch_shapes=[pltpu.VMEM((lines, LANE), jnp.float32), pltpu.SemaphoreType.DMA((PUTS, parts))],
         compiler_params=pltpu.CompilerParams(vmem_limit_bytes=16 * 1024 * 1024),
         name="put",
-    )(out)
+    )(vectors, columns)
     out = out.reshape(parts, ndate, blocks, rows, LANE).transpose(0, 1, 3, 2, 4)
     return out.reshape(parts, ndate, rows, cols)
 

time: 23.3 us -> 23.3 us (level)
  the two profiles are of different devices: /device:TPU:9 before, /device:TPU:11 now
where the time goes in v6:
time: 23.3 us; the launch traced here: 23.2 us
  Pallas kernels  22.5 us (97%)
  between operations  0.66 us (3%)
    pallas_call x1, Pallas kernels, per_device(): pl.pallas_call(body, out_shape=(jax.ShapeDtypeStruct((rows, blocks, depth...  21.4 us
    pallas_call x1, Pallas kernels, per_device(): pl.pallas_call(put, out_shape=jax.ShapeDtypeStruct((lines, LANE), jnp.flo...  1.14 us

profile of v6, /device:TPU:11, one launch (start us, length us, event | category | flops | bytes accessed | tf_op | source)
XLA Modules:
  0.0 23.2 jit_solution(440824112122265550)
XLA Ops:
  0.7 21.4 %link.1 = (f32[2,2,608,128]{3,2,1,0:T(8,128)S(1)}, f32[608,128]{1,0:T(8,128)S(1)}) custom-call(bf16[2400,128]{1,0:T(8,128)(2,1)} %bitcast.10, s32[25,2,256]{2,1,0:T(2,128)} %refs_1_.1, s32[1]{0:T(128)S(6)} %copy.6.refs_2_), custom_call_target="tpu_custom_call" | custom-call | tf_op jit(solution)/shard_map/link/pallas_call | solution.py:523
  22.0 1.1 %put.1 = f32[2400,128]{1,0:T(8,128)} custom-call(f32[2,2,608,128]{3,2,1,0:T(8,128)S(1)} %get-tuple-element.7.vectors, f32[608,128]{1,0:T(8,128)S(1)} %get-tuple-element.8.columns), custom_call_target="tpu_custom_call" | custom-call | tf_op jit(solution)/shard_map/put/pallas_call | solution.py:593

commit v7 on v6

--- a/solution.py
+++ b/solution.py
@@ -23,8 +23,8 @@
 
 def kernel(
     n, ndate, x_hbm, mask_hbm, index_hbm, vectors, columns,
-    raw, mask_ref, index_ref, wide, scene, turned, chosen, picks, pieces, weight, pairs, coef, late, edges, total, gains, long_gain, column, powers, plane_rows, whole_row, refs,
-    load_sem, mask_sem, index_sem, lane_sem, far_sem, near_sem, piece_sem, power_sem, plane_sem, whole_sem, ref_sem,
+    raw, mask_ref, index_ref, wide, scene, turned, chosen, picks, pieces, weight, pairs, coef, late, edges, total, gains, long_gain, column, powers, plane_rows, refs,
+    load_sem, mask_sem, index_sem, meet_sem, lane_sem, far_sem, near_sem, piece_sem, power_sem, plane_sem, ref_sem,
 ):
     _, rows, cols = mask_ref.shape
     span, blocks, depth, _ = scene.shape
@@ -68,6 +68,9 @@
     has_down = plane > 0
     crosses = has_far & ((lane + 1 - 2 * (1 - odd) < 0) | (lane + 1 - 2 * (1 - odd) > group - 1))
 
+    inner = (lane > 0) & (lane < group - 1) if planes > 1 else lane >= 0
+    outer = jnp.logical_not(inner)
+
     def signal(sem, target):
         pl.semaphore_signal(sem, inc=1, device_id={"row": target}, device_id_type=MESH)
 
@@ -77,10 +80,12 @@
 
     barrier = pltpu.get_barrier_semaphore()
     pl.when(crosses)(lambda: signal(barrier, jnp.clip(far, 0, n - 1)))
-    pl.when(has_up)(lambda: signal(barrier, jnp.minimum(me + group, n - 1)))
-    pl.when(has_down)(lambda: signal(barrier, jnp.maximum(me - group, 0)))
+    hub = me + inner.astype(jnp.int32) * (near - me)
+    pl.when(has_up)(lambda: signal(barrier, jnp.minimum(hub + group, n - 1)))
+    pl.when(has_down)(lambda: signal(barrier, jnp.maximum(hub - group, 0)))
     signal_mates(barrier)
-    expected = group - 1 + has_up.astype(jnp.int32) + has_down.astype(jnp.int32) + crosses.astype(jnp.int32)
+    others = 2 * has_up.astype(jnp.int32) + 2 * has_down.astype(jnp.int32) + crosses.astype(jnp.int32)
+    expected = group - 1 + outer.astype(jnp.int32) * others
 
     def meet_lane(d):
         pl.when(has_up)(lambda: signal(lane_sem.at[0, d], jnp.minimum(me + group, n - 1)))
@@ -150,6 +155,8 @@
         picks[slot] = found[0:EIGHT].astype(scene.dtype)
 
     pl.semaphore_wait(barrier, expected)
+    if planes > 1:
+        pl.when(outer)(lambda: signal(meet_sem, near))
 
     def mate_copy(k, rows_sent):
         return pltpu.make_async_remote_copy(
@@ -158,11 +165,12 @@
             device_id={"row": plane * group + lax.rem(lane + k, group)}, device_id_type=MESH,
         )
 
-    def plane_copy(k, rows_sent):
+    def plane_copy(k, rows_sent, aside):
+        target = lax.rem(plane + k, planes) * group + lane
         return pltpu.make_async_remote_copy(
             src_ref=plane_rows.at[rows_sent], dst_ref=plane_rows.at[rows_sent],
-            send_sem=plane_sem.at[0], recv_sem=plane_sem.at[1],
-            device_id={"row": lax.rem(plane + k, planes) * group + lane}, device_id_type=MESH,
+            send_sem=plane_sem.at[aside], recv_sem=plane_sem.at[2],
+            device_id={"row": target + aside * (near - me)}, device_id_type=MESH,
         )
 
     def ref_copy(k, rows_sent):
@@ -175,10 +183,8 @@
     mate_all = mate_copy(1, pl.ds(0, group - 1))
     ref_all = ref_copy(1, pl.ds(0, n - 1))
     if planes > 1:
-        plane_all = plane_copy(1, pl.ds(0, planes - 1))
-
-    inner = (lane > 0) & (lane < group - 1) if planes > 1 else lane >= 0
-    outer = jnp.logical_not(inner)
+        plane_all = [plane_copy(1, pl.ds(0, planes - 1), aside) for aside in range(2)]
+
 
     far_id = jnp.clip(far, 0, n - 1)
     near_id = jnp.clip(near, 0, n - 1)
@@ -222,10 +228,6 @@
         for t in range(1, HALF):
             far_copy(t).start()
 
-    whole_copy = pltpu.make_async_remote_copy(
-        src_ref=whole_row, dst_ref=whole_row, send_sem=whole_sem.at[0], recv_sem=whole_sem.at[1],
-        device_id={"row": near_id}, device_id_type=MESH,
-    )
     for k in range(1, group):
         mate_copy(k, lane).start()
     pl.when(inner & has_far)(far_first.start)
@@ -321,20 +323,15 @@
     if planes > 1:
         @pl.when(inner)
         def _():
+            pl.semaphore_wait(meet_sem, 1)
             for d in range(planes - 2):
                 meet_lane(d)
             for k in range(1, planes):
-                plane_copy(k, plane).start()
-            plane_all.wait_recv()
-            whole_row[...] = jnp.sum(plane_rows[...], axis=0)
-            whole_copy.start()
-
-        @pl.when(outer)
-        def _():
-            whole_copy.wait_recv()
-    else:
-        whole_row[...] = plane_rows[0]
-    power = whole_row[...]
+                for aside in range(2):
+                    plane_copy(k, plane, aside).start()
+
+        plane_all[0].wait_recv()
+    power = jnp.sum(plane_rows[...], axis=0)
     gain_row = lax.rsqrt(power * (1.0 / (total_rows * cols)) + 0.1)
     gains[...] = jnp.broadcast_to(gain_row, (LANE, long_dates)).T[0:half, :]
     tall = jnp.concatenate([gains[...], gains[...], jnp.zeros((long_depth - depth, LANE), jnp.float32)], axis=0)
@@ -494,8 +491,8 @@
     if planes > 1:
         @pl.when(inner)
         def _():
-            plane_all.wait_send()
-            whole_copy.wait_send()
+            plane_all[0].wait_send()
+            plane_all[1].wait_send()
 
 
 def per_device(slc, mask, ref_index):
@@ -549,18 +546,17 @@
             pltpu.VMEM((long_depth, LANE), jnp.float32),
             pltpu.VMEM((group, 1, long_dates), jnp.float32),
             pltpu.VMEM((n // group, 1, long_dates), jnp.float32),
-            pltpu.VMEM((1, long_dates), jnp.float32),
             pltpu.VMEM((n, 1, long_depth), jnp.float32),
             pltpu.SemaphoreType.DMA((2,)),
             pltpu.SemaphoreType.DMA,
             pltpu.SemaphoreType.DMA,
+            pltpu.SemaphoreType.REGULAR,
             pltpu.SemaphoreType.REGULAR((2, max(1, n // group - 2))),
             pltpu.SemaphoreType.DMA((HALF + 1,)),
             pltpu.SemaphoreType.DMA((2,)),
             pltpu.SemaphoreType.DMA((2,)),
             pltpu.SemaphoreType.DMA((2,)),
-            pltpu.SemaphoreType.DMA((2,)),
-            pltpu.SemaphoreType.DMA((2,)),
+            pltpu.SemaphoreType.DMA((3,)),
             pltpu.SemaphoreType.DMA((2,)),
         ],
         compiler_params=pltpu.CompilerParams(collective_id=0, has_side_effects=True, vmem_limit_bytes=VMEM_LIMIT),

time: 23.3 us -> 23.1 us (level)
  the two profiles are of different devices: /device:TPU:11 before, /device:TPU:25 now
where the time goes in v7:
time: 23.1 us; the launch traced here: 22.9 us
  Pallas kernels  22.3 us (97%)
  between operations  0.66 us (3%)
    pallas_call x1, Pallas kernels, per_device(): pl.pallas_call(body, out_shape=(jax.ShapeDtypeStruct((rows, blocks, depth...  21.1 us
    pallas_call x1, Pallas kernels, per_device(): pl.pallas_call(put, out_shape=jax.ShapeDtypeStruct((lines, LANE), jnp.flo...  1.14 us

profile of v7, /device:TPU:25, one launch (start us, length us, event | category | flops | bytes accessed | tf_op | source)
XLA Modules:
  0.0 22.9 jit_solution(4492957680847255282)
XLA Ops:
  0.7 21.1 %link.1 = (f32[2,2,608,128]{3,2,1,0:T(8,128)S(1)}, f32[608,128]{1,0:T(8,128)S(1)}) custom-call(bf16[2400,128]{1,0:T(8,128)(2,1)} %bitcast.10, s32[25,2,256]{2,1,0:T(2,128)} %refs_1_.1, s32[1]{0:T(128)S(6)} %copy.6.refs_2_), custom_call_target="tpu_custom_call" | custom-call | tf_op jit(solution)/shard_map/link/pallas_call | solution.py:520
  21.8 1.1 %put.1 = f32[2400,128]{1,0:T(8,128)} custom-call(f32[2,2,608,128]{3,2,1,0:T(8,128)S(1)} %get-tuple-element.7.vectors, f32[608,128]{1,0:T(8,128)S(1)} %get-tuple-element.8.columns), custom_call_target="tpu_custom_call" | custom-call | tf_op jit(solution)/shard_map/put/pallas_call | solution.py:589
